TPU v7x, 256 devices: a whole 4x4x8 slice. The times are simulated.
256 devices in a mesh: gx: 16 (over z, core), gy: 16 (over y, x).
Axes of the slice: x: 4, y: 4, z: 8, core: 2. Of those that a mesh axis runs over, the one named last changes fastest.
Arguments:
- bottom_in: bfloat16 [65536, 256], P(('gx', 'gy')), may hold values from -6 to 6
- bottom_pre: bfloat16 [65536, 128], P(('gx', 'gy')), may hold values from -6 to 6
- pooled: bfloat16 [65536, 2, 128], P(('gx', 'gy')), may hold values from -6 to 6
- top_pre: bfloat16 [65536, 1024], P(('gx', 'gy')), may hold values from -6 to 6
- top_cotangent: bfloat16 [65536, 1024], P(('gx', 'gy')), may hold values from -0.75 to 0.75
- top_weight: bfloat16 [384, 1024], replicated, may hold values from -0.5 to 0.5
- lookup_owner: int32 [65536, 2, 32], P(('gx', 'gy')), may hold values from 0 to 255, as said below
- lookup_row: int32 [65536, 2, 32], P(('gx', 'gy')), may hold values from 0 to 2047
Outputs:
- table_grad: float32 [2, 524288, 128], P(None, ('gx', 'gy'))
- top_weight_grad: float32 [384, 1024], P('gy')
- top_bias_grad: float32 [1024], P('gy')
- bottom_weight_grad: float32 [256, 128], P('gy')
Inputs may be any that keep to these rules, and one draw needn't show every extreme that they name: `lookup_owner`: row r of a table with r = owner * 2048 + row is held by device owner in the order of gx+gy. Among the lookups of one device's 256 bags and one table, every owner number appears at most 64 times, and one owner number, the same for all devices of that table, exactly 64 times.
All inputs are finite; a program needn't handle non-finite values.
Results may differ from a plain program's by a relative error of at most 0.003.
Values may be sent and summed in bfloat16 or wider, within the bound.
No kernel may reach another device: no remote copies, remote signals or barrier semaphores. Data moves between devices by JAX's collectives and lax.ppermute only.
A program may use at most 128 MiB of HBM per device.

v0:
```python
import math

import jax
import jax.numpy as jnp
from jax import lax
from jax.sharding import PartitionSpec as P

ROWS_DEV = 2048


def cut_along(x, dim, peers):
    before, after = (x.shape[:dim], x.shape[dim + 1 :])
    return jnp.moveaxis(x.reshape(*before, peers, -1, *after), dim, 0)


def joined_along(tiles, dim):
    tiles = jnp.moveaxis(tiles, 0, dim)
    shape = tiles.shape
    return tiles.reshape(*shape[:dim], shape[dim] * shape[dim + 1], *shape[dim + 2 :])


def one_exchange(x, axis, axes, splits, concats):
    sizes = [lax.axis_size(a) for a in axes]
    tiles = cut_along(x, splits[0], sizes[0])
    tiles = jnp.moveaxis(cut_along(tiles, splits[1] + 1, sizes[1]), 0, 1)
    inside = tiles.shape[2:]
    tiles = tiles.reshape(-1, *inside)
    tiles = lax.all_to_all(tiles, axis, split_axis=0, concat_axis=0, tiled=True)
    tiles = joined_along(tiles.reshape(*sizes, *inside), concats[0] + 1)
    return joined_along(tiles, concats[1])


def sum_together(arrays, axis, dims):
    peers = lax.axis_size(axis)
    tiles = [cut_along(a, dim, peers) for a, dim in zip(arrays, dims)]
    lines = jnp.concatenate([b.reshape(peers, -1) for b in tiles], axis=1)
    span = max(16, -(-lines.shape[1] // 1024) * 8)
    lines = jnp.pad(lines, ((0, 0), (0, span * 128 - lines.shape[1]))).reshape(-1, 128)
    line, at, outs = (lax.psum_scatter(lines, axis, tiled=True).reshape(-1), 0, [])
    for b in tiles:
        part = b[0]
        outs.append(line[at : at + part.size].reshape(part.shape))
        at += part.size
    return tuple(outs)


def copy_for_each(x, axis):
    copies = jnp.broadcast_to(x, (lax.axis_size(axis), *x.shape))
    return lax.all_to_all(copies, axis, split_axis=0, concat_axis=0, tiled=True)


def of_everyone(x, axis):
    everything = copy_for_each(x, axis)
    return jnp.sum(everything, axis=0)


def in_one(arrays, axis):
    line, at, outs = (jnp.concatenate([a.reshape(-1) for a in arrays]), 0, [])
    total = of_everyone(line, axis)
    for a in arrays:
        outs.append(total[at : at + a.size].reshape(a.shape))
        at += a.size
    return tuple(outs)


def slot_positions(owner_lists, devices):
    tables, lookups = owner_lists.shape
    member = (
        owner_lists[:, :, None] == jnp.arange(devices, dtype=jnp.int32)[None, None, :]
    ).astype(jnp.bfloat16)
    block = math.gcd(lookups, 512)
    blocks = lookups // block
    member_blocks = member.reshape(tables, blocks, block, devices)
    lower = (
        jnp.arange(block, dtype=jnp.int32)[:, None] > jnp.arange(block, dtype=jnp.int32)[None, :]
    ).astype(jnp.bfloat16)
    within = jnp.einsum("ik,tnkv->tniv", lower, member_blocks, preferred_element_type=jnp.float32)
    member_float = member_blocks.astype(jnp.float32)
    totals = jnp.sum(member_float, axis=2)
    offsets = jnp.cumsum(totals, axis=1) - totals
    before = within + offsets[:, :, None, :]
    return jnp.sum(before * member_float, axis=3).reshape(tables, lookups).astype(jnp.int32)


def shards(
    bottom_in, bottom_pre, pooled, top_pre, top_cotangent, top_weight, lookup_owner, lookup_row
):
    bag_count = bottom_in.shape[0]
    tables = pooled.shape[1]
    feature_width = pooled.shape[2]
    bag_size = lookup_owner.shape[2]
    top_grad = jnp.where(top_pre > 0, top_cotangent, jnp.zeros_like(top_cotangent))
    bottom_out = jnp.maximum(bottom_pre, jnp.zeros_like(bottom_pre))
    feature = jnp.concatenate(
        [bottom_out, pooled.reshape(bag_count, tables * feature_width)], axis=1
    )
    top_weight_part = lax.dot_general(
        feature, top_grad, (((0,), (0,)), ((), ())), preferred_element_type=jnp.float32
    )
    top_bias_part = jnp.sum(top_grad.astype(jnp.float32), axis=0)
    feature_grad = lax.dot_general(
        top_grad, top_weight, (((1,), (1,)), ((), ())), preferred_element_type=jnp.float32
    ).astype(jnp.bfloat16)
    bottom_grad = jnp.where(
        bottom_pre > 0, feature_grad[:, :feature_width], jnp.zeros_like(bottom_pre)
    )
    bottom_weight_part = lax.dot_general(
        bottom_in, bottom_grad, (((0,), (0,)), ((), ())), preferred_element_type=jnp.float32
    )
    bag_grad = feature_grad[:, feature_width:].reshape(bag_count, tables, feature_width)
    gx_count = lax.axis_size("gx")
    gy_count = lax.axis_size("gy")
    devices = gx_count * gy_count
    capacity = max(2, 2 * bag_count * bag_size // devices)
    local_rows = ROWS_DEV
    slot_total = devices * capacity
    owner_lists = lookup_owner.transpose(1, 0, 2).reshape(tables, bag_count * bag_size)
    positions = slot_positions(owner_lists, devices)
    slot_keys = owner_lists * capacity + positions
    table_index = jnp.broadcast_to(jnp.arange(tables, dtype=jnp.int32)[:, None], slot_keys.shape)
    values = jnp.broadcast_to(
        bag_grad.transpose(1, 0, 2)[:, :, None, :], (tables, bag_count, bag_size, feature_width)
    )
    values = values.reshape(tables, bag_count * bag_size, feature_width)
    row_values = lookup_row.transpose(1, 0, 2).reshape(tables, bag_count * bag_size)
    outgoing = (
        jnp.zeros((slot_total, tables, feature_width), jnp.bfloat16)
        .at[slot_keys, table_index]
        .set(values)
    )
    outgoing_rows = (
        jnp.full((slot_total, tables), local_rows, jnp.int32)
        .at[slot_keys, table_index]
        .set(row_values)
    )
    outgoing = outgoing.reshape(gx_count, gy_count, capacity, tables, feature_width)
    outgoing_rows = outgoing_rows.reshape(gx_count, gy_count, capacity, tables)
    incoming, incoming_rows = (
        one_exchange(outgoing, ("gx", "gy"), ("gx", "gy"), (0, 1), (0, 1)),
        one_exchange(outgoing_rows, ("gx", "gy"), ("gx", "gy"), (0, 1), (0, 1)),
    )
    incoming = incoming.reshape(slot_total, tables, feature_width)
    incoming_rows = incoming_rows.reshape(slot_total, tables)
    receive_tables = jnp.broadcast_to(
        jnp.arange(tables, dtype=jnp.int32)[None, :], incoming_rows.shape
    )
    padded_grad = jnp.zeros((tables, local_rows + 1, feature_width), jnp.float32)
    padded_grad = padded_grad.at[receive_tables, incoming_rows].add(incoming.astype(jnp.float32))
    table_grad = padded_grad[:, :local_rows, :]
    shares = sum_together((top_weight_part, top_bias_part, bottom_weight_part), "gy", (0, 0, 0))
    top_weight_grad, top_bias_grad, bottom_weight_grad = in_one(
        (shares[0], shares[1], shares[2]), "gx"
    )
    return (table_grad, top_weight_grad, top_bias_grad, bottom_weight_grad)


def solution(mesh):
    return jax.shard_map(
        shards,
        mesh=mesh,
        in_specs=(
            P(("gx", "gy"), None),
            P(("gx", "gy"), None),
            P(("gx", "gy"), None, None),
            P(("gx", "gy"), None),
            P(("gx", "gy"), None),
            P(),
            P(("gx", "gy"), None, None),
            P(("gx", "gy"), None, None),
        ),
        out_specs=(P(None, ("gx", "gy"), None), P("gy", None), P("gy"), P("gy", None)),
        check_vma=False,
    )
```

profile of v0, /device:TPU:1, one launch (start us, length us, event | category | flops | bytes accessed | tf_op | source)
XLA Modules:
  0.0 572.5 jit_solution(13361391412937839239)
XLA Ops:
  7.2 0.0 copy-start
  7.2 0.0 all-reduce.4.cloned.1.call-start
  7.2 1.5 convert_reduce_fusion.1
  8.7 0.1 reshape.164
  8.8 0.8 broadcast_maximum_fusion
  9.6 0.9 copy.65
  10.5 1.7 convolution_convert_fusion
  12.2 1.1 convolution_bitcast_fusion
  13.3 0.1 copy.50
  13.5 2.8 fusion.11
  16.3 1.7 reshape_reshape.11
  18.0 1.4 concatenate.20
  19.4 1.6 pad.4
  21.0 1.5 reshape.165
  22.5 0.0 all-reduce.4.cloned.1.call-update
  22.5 0.1 copy.43
  22.6 0.2 mul.21
  22.8 0.1 copy.45
  22.9 0.1 reshape.186
  23.1 0.1 copy.44
  23.2 0.1 eq.17
  23.3 1.8 convert_reduce_fusion
  25.2 0.0 copy-start.7
  25.2 0.0 copy-start.5
  25.2 7.6 %fusion = f32[2,16,512]{2,1,0:T(8,128)S(1)} fusion(f32[2,16,256]{2,1,0:T(8,128)S(1)} %sub.7, s32[2,16,512]{2,1,0:T(8,128)S(1)} %eq.17), kind=kOutput, calls=%fused_computation.5 | convolution fusion | flops 4324573184 | bytes 163840 | tf_op jit(solution)/shard_map/ik,tnkv->tniv/dot_general | solution.py:77
  32.8 0.1 convert_element_type.47
  32.9 0.1 compare_select_fusion.2
  33.0 0.2 and_reduce_fusion.1
  33.2 0.2 multiply_reduce_fusion.1
  33.4 0.1 select_bitcast_fusion
  33.5 60.4 %scatter_custom_fusion = s32[32768]{0:T(1024)S(1)} fusion(s32[16384]{0:T(1024)S(1)} %bitcast.81, s32[16384]{0:T(1024)S(1)} %reshape.186, s32[]{:T(128)} %constant.8.clone.1), kind=kCustom, calls=%fused_computation.41 | custom fusion | bytes 131076
  93.9 0.1 reshape.171
  94.0 0.2 reshape_transpose_transpose_reshape_reshape_reshape.6
  94.2 0.2 copy.66
  94.4 0.9 reshape.214
  95.3 15.6 %all-to-all-start = ((s32[256,1,128]{2,1,0:T(1,128)}), s32[256,1,128]{2,1,0:T(1,128)S(1)}, u32[]{:S(2)}, u32[]{:S(2)}) async-start(s32[256,1,128]{2,1,0:T(1,128)} %reshape.214), calls=%async_computation | async-start | bytes 262144 | tf_op jit(solution)/shard_map/all_to_all | solution.py:28
  111.0 0.6 dynamic-slice
  112.2 12.9 %all-reduce.4.cloned.1.call-done = f32[3456,128]{1,0:T(8,128)} async-done(((f32[3456,128]{1,0:T(8,128)}), f32[3456,128]{1,0:T(8,128)}) %all-reduce.4.cloned.1.call-update) | async-done | bytes 1769488
  125.1 0.9 dynamic-slice_bitcast_fusion
  126.1 0.9 dynamic-slice_bitcast_fusion.1
  127.0 2.1 broadcast_in_dim.20
  129.1 8.7 %all-to-all-start.2 = ((f32[16,1,26688]{2,1,0:T(1,128)}), f32[16,1,26688]{2,1,0:T(1,128)S(1)}, u32[]{:S(2)}, u32[]{:S(2)}) async-start(f32[16,1,26688]{2,1,0:T(1,128)} %broadcast_in_dim.20), calls=%async_computation.2 | async-start | bytes 3424256 | tf_op jit(solution)/shard_map/all_to_all | solution.py:49
  137.8 2.5 broadcast_in_dim.19
  140.3 46.3 %scatter_custom_fusion.1 = bf16[32768,128]{1,0:T(8,128)(2,1)} fusion(s32[16384]{0:T(1024)S(1)} %bitcast.80, bf16[16384,128]{1,0:T(8,128)(2,1)} %bitcast.70, bf16[]{:T(256)} %constant.13.clone.1), kind=kCustom, calls=%fused_computation.12 | custom fusion | bytes 8389120
  186.6 12.0 %all-to-all-start.1 = ((bf16[256,1,1,64,2,128]{5,4,3,2,1,0:T(2,128)(2,1)}), bf16[256,1,1,64,2,128]{5,4,3,2,1,0:T(2,128)(2,1)}, u32[]{:S(2)}, u32[]{:S(2)}) async-start(bf16[256,1,1,64,2,128]{5,4,3,2,1,0:T(2,128)(2,1)} %bitcast.68), calls=%async_computation.1 | async-start | bytes 16777216 | tf_op jit(solution)/shard_map/all_to_all | solution.py:28
  198.6 0.5 broadcast.158
  199.1 1.0 reduce.12
  200.1 0.2 reshape.215
  200.3 0.1 reshape_reshape.10
  200.4 0.1 compare_select_fusion.1
  200.6 0.2 multiply_reduce_fusion
  200.8 0.3 and_reduce_fusion
  201.1 0.1 broadcast_select_fusion
  201.2 5.0 copy.48
  206.2 6.9 %reshape.196 = s32[32768]{0:T(1024)S(1)} reshape(s32[16384,2]{1,0:T(8,128)} %copy.48) | data formatting | bytes 262144
  213.1 1.1 reduce_sum.39
  214.2 0.5 slice.43
  214.7 0.7 reshape.167
  215.4 0.7 slice_bitcast_fusion
  216.0 168.1 %all-to-all-done.1 = bf16[256,1,1,64,2,128]{5,4,3,2,1,0:T(2,128)(2,1)} async-done(((bf16[256,1,1,64,2,128]{5,4,3,2,1,0:T(2,128)(2,1)}), bf16[256,1,1,64,2,128]{5,4,3,2,1,0:T(2,128)(2,1)}, u32[]{:S(2)}, u32[]{:S(2)}) %all-to-all-start.1) | async-done | bytes 8388640 | tf_op jit(solution)/shard_map/all_to_all | solution.py:28
  384.1 175.8 %scatter_custom_fusion.2 = f32[4098,128]{1,0:T(8,128)S(1)} fusion(s32[32768]{0:T(1024)S(1)} %reshape.196, bf16[32768,128]{1,0:T(8,128)(2,1)} %bitcast.32, f32[]{:T(128)} %constant.7.clone.1), kind=kCustom, calls=%fused_computation.6 | custom fusion | flops 8388608 | bytes 10486788
  560.0 2.6 reshape.179
  562.6 1.6 slice.39
  564.2 1.5 copy.52
  (33 shorter events, 0.3 us)
Async XLA Ops:
  7.2 3.4 copy-start
  7.2 118.0 %all-reduce.4.cloned.1.call-start = ((), (), s32[]{:S(2)}) async-start(), calls=%async_computation.3 | async-start | bytes 3538944
  13.5 9.0 %copy-start.1 = (s32[256,2,32]{0,2,1:T(8,128)S(1)}, s32[256,2,32]{0,2,1:T(8,128)}, u32[]{:S(2)}) copy-start(s32[256,2,32]{0,2,1:T(8,128)} %param.14) | copy-start | bytes 196612
  16.3 6.5 %copy-start.2 = (s32[256,2,32]{0,2,1:T(8,128)S(1)}, s32[256,2,32]{0,2,1:T(8,128)}, u32[]{:S(2)}) copy-start(s32[256,2,32]{0,2,1:T(8,128)} %param.15) | copy-start | bytes 196612
  25.2 7.8 %copy-start.7 = (s32[2]{0:T(128)S(1)}, s32[2]{0:T(128)}, u32[]{:S(2)}) copy-start(s32[2]{0:T(128)} %constant.32) | copy-start | bytes 28
  25.2 8.0 %copy-start.5 = (s32[2]{0:T(128)S(1)}, s32[2]{0:T(128)}, u32[]{:S(2)}) copy-start(s32[2]{0:T(128)} %constant.35) | copy-start | bytes 28
  25.2 8.0 %copy-start.6 = (s32[2]{0:T(128)S(1)}, s32[2]{0:T(128)}, u32[]{:S(2)}) copy-start(s32[2]{0:T(128)} %constant.14) | copy-start | bytes 28
  25.2 85.8 %copy-start.8 = (u32[256]{0:T(256)S(1)}, u32[256]{0:T(256)}, u32[]{:S(2)}) copy-start(u32[256]{0:T(256)} %constant.53) | copy-start | bytes 3076
  95.3 31.7 %all-to-all-start = ((s32[256,1,128]{2,1,0:T(1,128)}), s32[256,1,128]{2,1,0:T(1,128)S(1)}, u32[]{:S(2)}, u32[]{:S(2)}) async-start(s32[256,1,128]{2,1,0:T(1,128)} %reshape.214), calls=%async_computation | async-start | bytes 262144 | tf_op jit(solution)/shard_map/all_to_all | solution.py:28
  129.1 57.5 %all-to-all-start.2 = ((f32[16,1,26688]{2,1,0:T(1,128)}), f32[16,1,26688]{2,1,0:T(1,128)S(1)}, u32[]{:S(2)}, u32[]{:S(2)}) async-start(f32[16,1,26688]{2,1,0:T(1,128)} %broadcast_in_dim.20), calls=%async_computation.2 | async-start | bytes 3424256 | tf_op jit(solution)/shard_map/all_to_all | solution.py:49
  186.6 14.0 %copy-start.4 = (s32[2]{0:T(128)S(1)}, s32[2]{0:T(128)}, u32[]{:S(2)}) copy-start(s32[2]{0:T(128)} %constant.41) | copy-start | bytes 28
  186.6 14.2 %copy-start.3 = (s32[2]{0:T(128)S(1)}, s32[2]{0:T(128)}, u32[]{:S(2)}) copy-start(s32[2]{0:T(128)} %constant.44) | copy-start | bytes 28
  186.6 197.5 %all-to-all-start.1 = ((bf16[256,1,1,64,2,128]{5,4,3,2,1,0:T(2,128)(2,1)}), bf16[256,1,1,64,2,128]{5,4,3,2,1,0:T(2,128)(2,1)}, u32[]{:S(2)}, u32[]{:S(2)}) async-start(bf16[256,1,1,64,2,128]{5,4,3,2,1,0:T(2,128)(2,1)} %bitcast.68), calls=%async_computation.1 | async-start | bytes 16777216 | tf_op jit(solution)/shard_map/all_to_all | solution.py:28
Sparse Core Ops, SparseCore 0:
  22.6 102.4 all-reduce.3
where the time goes:
time: 573 us
  other arithmetic  183 us (32%)
  waiting for transfers between devices  181 us (32%)
  local copies, waits for them, and re-layouts  144 us (25%)
  starting transfers between devices  36.3 us (6%)
  between operations  15.1 us (3%)
  matrix products  13.2 us (2%)
    unnamed x7, other arithmetic  177 us
    all_to_all x2, waiting for transfers between devices, one_exchange(): tiles = lax.all_to_all(tiles, axis, split_axis=0, concat_axis=0, tiled=True)  168 us
    unnamed x31, local copies, waits for them, and re-layouts  125 us
    all_to_all x2, starting transfers between devices, one_exchange(): tiles = lax.all_to_all(tiles, axis, split_axis=0, concat_axis=0, tiled=True)  27.6 us
    unnamed x2, waiting for transfers between devices  12.9 us
  transfers between devices with their start and end apart: 4, of which 2 were waited for; matrix products, arithmetic and copies ran while one was open for 25% of the time, Pallas kernels for 0%

commit v1 on v0

v1 whole, which is shorter than its diff:
```python
import functools

import jax
import jax.numpy as jnp
from jax import lax
from jax.experimental import pallas as pl
from jax.experimental.pallas import tpu as pltpu
from jax.sharding import PartitionSpec as P


ROWS_DEV = 2048
CAP = 64
CORES = 2
SIDE = 4
GROUP = 8
PEERS = 2
FREE = 256
BAG_STEP = 4096
NT = (((1,), (1,)), ((), ()))
NN = (((1,), (0,)), ((), ()))


def exchange(x, axis):
    return lax.all_to_all(x, axis, split_axis=0, concat_axis=0, tiled=True)


def slot_kernel(owner_ref, row_ref, code_ref, member, column):
    tables, lookups, bags = owner_ref.shape
    owners = code_ref.shape[0]
    owner_ids = lax.broadcasted_iota(jnp.int32, (owners, bags), 0)
    slot_ids = lax.broadcasted_iota(jnp.int32, (CAP, bags), 0)
    bag_ids = lax.broadcasted_iota(jnp.int32, (CAP, bags), 1).astype(jnp.float32)
    earlier = (
        lax.broadcasted_iota(jnp.int32, (bags, bags), 0)
        < lax.broadcasted_iota(jnp.int32, (bags, bags), 1)
    ).astype(jnp.bfloat16)
    for t in range(tables):
        counts = jnp.zeros((owners, bags), jnp.float32)
        for j in range(lookups):
            hit = owner_ref[t, j : j + 1, :] == owner_ids
            counts = counts + jnp.where(hit, 1.0, 0.0)
        taken = lax.dot_general(
            counts.astype(jnp.bfloat16), earlier, NN, preferred_element_type=jnp.float32
        )
        for j in range(lookups):
            span = slice(j * bags, (j + 1) * bags)
            hit = owner_ref[t, j : j + 1, :] == owner_ids
            rank = jnp.sum(jnp.where(hit, taken, 0.0), axis=0, keepdims=True)
            one = jnp.where(hit, 1.0, 0.0)
            taken = taken + one
            member[:, span] = one.astype(jnp.bfloat16)
            place = rank.astype(jnp.int32) == slot_ids
            row = row_ref[t, j : j + 1, :] + FREE
            high = (row >> 8).astype(jnp.float32)
            low = (row & 255).astype(jnp.float32)
            column[0:CAP, span] = jnp.where(place, bag_ids, 0.0).astype(jnp.bfloat16)
            column[CAP : 2 * CAP, span] = jnp.where(place, high, 0.0).astype(jnp.bfloat16)
            column[2 * CAP : 3 * CAP, span] = jnp.where(place, low, 0.0).astype(jnp.bfloat16)
        found = lax.dot_general(member[...], column[...], NT, preferred_element_type=jnp.float32)
        code = (
            found[:, 0:CAP] * float(BAG_STEP)
            + found[:, CAP : 2 * CAP] * 256.0
            + found[:, 2 * CAP : 3 * CAP]
        )
        code_ref[:, t * CAP : (t + 1) * CAP] = code.astype(jnp.int32)


def slot_codes(owner_lists, row_lists, owners):
    tables, lookups, bags = owner_lists.shape
    return pl.pallas_call(
        slot_kernel,
        out_shape=jax.ShapeDtypeStruct((owners, tables * CAP), jnp.int32),
        scratch_shapes=[
            pltpu.VMEM((owners, lookups * bags), jnp.bfloat16),
            pltpu.VMEM((3 * CAP, lookups * bags), jnp.bfloat16),
        ],
        cost_estimate=pl.CostEstimate(
            flops=4 * 10**9, bytes_accessed=262144, transcendentals=0
        ),
        name="slots",
    )(owner_lists, row_lists)


def tall(row, height):
    return jnp.tile(jnp.broadcast_to(row, (16, row.shape[1])).astype(jnp.bfloat16), (height // 16, 1))


def paired(mine, other, lane, t):
    if t == 0:
        return jnp.where(lane < CAP, mine, pltpu.roll(other, CAP, 1))
    return jnp.where(lane < CAP, pltpu.roll(mine, CAP, 1), other)


def gather_kernel(_, mine_ref, other_ref, mine_grad, other_grad, out_ref):
    tables, width, bags = mine_grad.shape[1:]
    peers, lanes = mine_ref.shape[1:]
    mine, other = mine_ref[0], other_ref[0]
    lane = lax.broadcasted_iota(jnp.int32, (peers, lanes), 1)
    group = GROUP * lanes
    bag_ids = lax.broadcasted_iota(jnp.int32, (bags, group), 0).astype(jnp.float32)
    bag_ids = bag_ids.astype(jnp.bfloat16)
    one = jnp.ones((), jnp.bfloat16)
    zero = jnp.zeros((), jnp.bfloat16)
    first = (lax.broadcasted_iota(jnp.int32, (width, group), 1) & (lanes - 1)) < CAP
    line = lax.broadcasted_iota(jnp.int32, (16, lanes), 0)
    keys = [jnp.zeros((16, lanes), jnp.float32) for _ in range(peers)]
    for t in range(tables):
        code = paired(mine, other, lane, t)
        bag = (code >> 12).astype(jnp.float32)
        row = code & (BAG_STEP - 1)
        high = (row >> 8).astype(jnp.float32)
        low = (row & 255).astype(jnp.float32)
        both = jnp.concatenate([mine_grad[0, t], other_grad[0, t]], axis=0)
        span = slice(t * width, (t + 1) * width)
        for y in range(0, peers, GROUP):
            wanted = jnp.concatenate([bag[y + u : y + u + 1] for u in range(GROUP)], axis=1)
            pick = jnp.where(bag_ids == tall(wanted, bags), one, zero)
            got = lax.dot_general(both, pick, NN, preferred_element_type=jnp.float32)
            value = jnp.where(first, got[:width], got[width:]).astype(jnp.bfloat16)
            for u in range(GROUP):
                out_ref[y + u, span, :] = value[:, u * lanes : (u + 1) * lanes]
        for y in range(peers):
            keys[y] = jnp.where(line == 2 * t, high[y : y + 1], keys[y])
            keys[y] = jnp.where(line == 2 * t + 1, low[y : y + 1], keys[y])
    for y in range(peers):
        out_ref[y, tables * width :, :] = keys[y].astype(jnp.bfloat16)


def gathered(order, codes, mine, other):
    steps, tables, width, bags = mine.shape
    peers, lanes = codes.shape[1:]
    rows = tables * width + 16
    return pl.pallas_call(
        gather_kernel,
        grid_spec=pltpu.PrefetchScalarGridSpec(
            num_scalar_prefetch=1,
            grid=(steps,),
            in_specs=[
                pl.BlockSpec((1, peers, lanes), lambda i, order: (order[0, i], 0, 0)),
                pl.BlockSpec((1, peers, lanes), lambda i, order: (order[1, i], 0, 0)),
                pl.BlockSpec((1, tables, width, bags), lambda i, order: (i, 0, 0, 0)),
                pl.BlockSpec((1, tables, width, bags), lambda i, order: (i, 0, 0, 0)),
            ],
            out_specs=pl.BlockSpec((peers, rows, lanes), lambda i, order: (0, 0, i)),
        ),
        out_shape=jax.ShapeDtypeStruct((peers, rows, 2 * steps * CAP), jnp.bfloat16),
        cost_estimate=pl.CostEstimate(
            flops=8 * 10**9, bytes_accessed=12 * 2**20, transcendentals=0
        ),
        name="gather",
    )(order, codes, codes, mine, other)


def scatter_kernel(t, *refs):
    value_ref, key_ref, out_ref, total = refs[0], refs[1], refs[-2], refs[-1]
    peers, width, slots = value_ref.shape
    quarter = 256
    half = ROWS_DEV // 2
    step = pl.program_id(0)

    @pl.when(step == 0)
    def _():
        total[...] = jnp.zeros_like(total)

    row_ids = lax.broadcasted_iota(jnp.int32, (quarter, slots), 0).astype(jnp.float32)
    row_ids = row_ids.astype(jnp.bfloat16)
    one = jnp.ones((), jnp.bfloat16)
    zero = jnp.zeros((), jnp.bfloat16)
    hits, spreads = [], []
    for p in range(peers):
        keys = key_ref[p].astype(jnp.float32)
        high = keys[2 * t : 2 * t + 1] - 1.0
        low = keys[2 * t + 1 : 2 * t + 2]
        lower = tall(jnp.where(high < 4.0, 1.0, 0.0), width)
        upper = tall(jnp.where(high < 4.0, 0.0, 1.0), width)
        value = value_ref[p]
        spreads.append(jnp.concatenate([value * lower, value * upper], axis=0))
        parts = []
        for k in range(half // quarter):
            here = (high == float(k)) | (high == float(k + 4))
            key = tall(jnp.where(here, low, -1.0), quarter)
            parts.append(jnp.where(row_ids == key, one, zero))
        hits.append(jnp.concatenate(parts, axis=0))
    total[...] += lax.dot_general(
        jnp.concatenate(hits, axis=1),
        jnp.concatenate(spreads, axis=1),
        NT,
        preferred_element_type=jnp.float32,
    )

    @pl.when(step == pl.num_programs(0) - 1)
    def _():
        out_ref[0, :half, :] = total[:, :width]
        out_ref[0, half:, :] = total[:, width:]


def scattered(t, tables, values, width, before):
    peers, _, slots = values.shape
    in_specs = [
        pl.BlockSpec((PEERS, width, slots), lambda i: (i, t, 0)),
        pl.BlockSpec((PEERS, 16, slots), lambda i: (i, tables * width // 16, 0)),
    ]
    args = [values, values]
    aliases = {}
    if before is not None:
        in_specs.append(pl.BlockSpec(memory_space=pl.ANY))
        args.append(before)
        aliases = {2: 0}
    return pl.pallas_call(
        functools.partial(scatter_kernel, t),
        grid=(peers // PEERS,),
        in_specs=in_specs,
        out_specs=pl.BlockSpec((1, ROWS_DEV, width), lambda i: (t, 0, 0)),
        out_shape=jax.ShapeDtypeStruct((tables, ROWS_DEV, width), jnp.float32),
        scratch_shapes=[pltpu.VMEM((ROWS_DEV // 2, 2 * width), jnp.float32)],
        input_output_aliases=aliases,
        cost_estimate=pl.CostEstimate(
            flops=2 * 10**10, bytes_accessed=6 * 2**20, transcendentals=0
        ),
        name="scatter",
    )(*args)


def passed(part, place, dim, target, devices):
    peers = part.shape[dim]
    total = lax.dynamic_index_in_dim(part, place, dim, keepdims=False)
    for k in range(1, peers):
        give = lax.dynamic_index_in_dim(part, (place + k) % peers, dim, keepdims=False)
        total = total + lax.ppermute(give, "gy", [(i, target(i, k)) for i in range(devices)])
    return total


def body(
    bottom_in, bottom_pre, pooled, top_pre, top_cotangent, top_weight, lookup_owner, lookup_row
):
    bags, tables, width = pooled.shape
    gx = lax.axis_size("gx")
    gy = lax.axis_size("gy")
    f32 = jnp.float32
    bf16 = jnp.bfloat16
    me = lax.axis_index("gx")
    chips = gx // CORES
    columns = [[z * CORES + c for z in range(chips)] for c in range(CORES)]

    owner_lists = lookup_owner.transpose(1, 2, 0)
    row_lists = lookup_row.transpose(1, 2, 0)
    codes = slot_codes(owner_lists, row_lists, gx * gy)
    codes = exchange(codes.reshape(gx, gy, tables * CAP), "gx")
    chip = jnp.arange(chips, dtype=jnp.int32)
    order = jnp.stack(
        [chip * CORES + (me & 1), chip * CORES + (1 - (me & 1))]
    ).astype(jnp.int32)

    top_grad = jnp.where(top_pre > 0, top_cotangent, jnp.zeros_like(top_cotangent))
    grad = lax.dot_general(top_weight[width:], top_grad, NT, preferred_element_type=f32)
    grad = grad.astype(bf16).reshape(tables, width, bags)
    copies = jnp.broadcast_to(grad, (chips, tables, width, bags))
    mine = lax.all_to_all(
        copies, "gx", split_axis=0, concat_axis=0, axis_index_groups=columns, tiled=True
    )
    other = lax.ppermute(mine, "gx", [(i, i ^ 1) for i in range(gx)])
    payload = gathered(order, codes, mine, other)

    bottom_out = jnp.maximum(bottom_pre, jnp.zeros_like(bottom_pre))
    feature = jnp.concatenate([bottom_out, pooled.reshape(bags, tables * width)], axis=1)
    first = lax.dot_general(top_grad, top_weight[:width], NT, preferred_element_type=f32)
    bottom_grad = jnp.where(bottom_pre > 0, first.astype(bf16), jnp.zeros_like(bottom_pre))
    top_part = lax.dot_general(
        feature, top_grad, (((0,), (0,)), ((), ())), preferred_element_type=f32
    )
    bias_part = jnp.sum(top_grad.astype(f32), axis=0)
    bottom_part = lax.dot_general(
        bottom_in, bottom_grad, (((0,), (0,)), ((), ())), preferred_element_type=f32
    )
    top_in, top = top_part.shape
    bottom_width = bottom_part.shape[0]
    top_rows = top_in // gy
    bottom_rows = bottom_width // gy * width // top
    tail = jnp.concatenate(
        [
            bottom_part.reshape(gy, bottom_rows, top),
            jnp.pad(bias_part.reshape(gy, 1, top // gy), ((0, 0), (0, 0), (0, top - top // gy))),
        ],
        axis=1,
    )
    tail = jnp.pad(tail, ((0, 0), (0, 8 - tail.shape[1]), (0, 0)))
    part = jnp.concatenate([top_part.reshape(gy, top_rows, top), tail], axis=1)
    half = part.shape[1] // CORES
    keep = lax.dynamic_slice_in_dim(part, (me & 1) * half, half, 1)
    give = lax.dynamic_slice_in_dim(part, (1 - (me & 1)) * half, half, 1)
    part = keep + lax.ppermute(give, "gx", [(i, i ^ 1) for i in range(gx)])
    part = part.reshape(gy // SIDE, SIDE, half, top)
    place = lax.axis_index("gy")
    part = passed(part, place % SIDE, 1, lambda i, k: i // SIDE * SIDE + (i + k) % SIDE, gy)
    part = passed(part, place // SIDE, 0, lambda i, k: (i + k * SIDE) % gy, gy)
    payload, part = lax.optimization_barrier((payload, part))
    arrived = exchange(payload, "gy")
    part, arrived = lax.optimization_barrier((part, arrived))

    part = lax.all_to_all(
        part.reshape(chips, half // chips, top),
        "gx", split_axis=0, concat_axis=0, axis_index_groups=columns, tiled=True,
    )
    part = jnp.sum(part, axis=0)
    total = exchange(jnp.broadcast_to(part, (gx, *part.shape)), "gx")
    total = total.reshape(chips, CORES, *part.shape).transpose(1, 0, 2, 3).reshape(-1, top)
    top_weight_grad = total[:top_rows]
    bottom_weight_grad = total[top_rows : top_rows + bottom_rows].reshape(-1, width)
    top_bias_grad = total[top_rows + bottom_rows, : top // gy]

    table_grad = None
    for t in range(tables):
        table_grad = scattered(t, tables, arrived, width, table_grad)
    return (table_grad, top_weight_grad, top_bias_grad, bottom_weight_grad)


def solution(mesh):
    return jax.shard_map(
        body,
        mesh=mesh,
        in_specs=(
            P(("gx", "gy"), None),
            P(("gx", "gy"), None),
            P(("gx", "gy"), None, None),
            P(("gx", "gy"), None),
            P(("gx", "gy"), None),
            P(),
            P(("gx", "gy"), None, None),
            P(("gx", "gy"), None, None),
        ),
        out_specs=(P(None, ("gx", "gy"), None), P("gy", None), P("gy"), P("gy", None)),
        check_vma=False,
    )
```

time: 573 us -> 231 us (0.40)
  other arithmetic: 183 us -> 3.77 us
  waiting for transfers between devices: 181 us -> 23.8 us
  local copies, waits for them, and re-layouts: 144 us -> 5.46 us
  blocking collectives: 0 us -> 109 us
  Pallas kernels: 0 us -> 46.7 us
  between operations: 15.1 us -> 0.93 us
  matrix products: 13.2 us -> 3.26 us
    unnamed x7 -> x0, other arithmetic: 177 us -> none
    all_to_all x3 -> x4, waiting for transfers between devices: 168 us -> 18.6 us  [the longest x1 17.5 us: body(): lax.all_to_all(copies, 'gx', split_axis=0, concat_axis=0, axis_index_grou...]
    unnamed x31 -> x9, local copies, waits for them, and re-layouts: 125 us -> 0.69 us
    all_to_all x0 -> x1, blocking collectives: none -> 109 us  [exchange(): return lax.all_to_all(x, axis, split_axis=0, concat_axis=0, tiled=True)]
    pallas_call x0 -> x4, Pallas kernels: none -> 46.7 us  [the longest x2 25.4 us: scattered(): pl.pallas_call(functools.partial(scatter_kernel, t), grid=(peers // PEERS...]
    unnamed x2 -> x0, waiting for transfers between devices: 12.9 us -> none
    ppermute x0 -> x8, starting transfers between devices: none -> 10.3 us  [the longest x6 8.74 us: passed(): lax.ppermute(give, 'gy', [(i, target(i, k)) for i in range(devices)])]
    dot_general x4 -> x3, matrix products: 13.2 us -> 3.26 us  [the longest x1 1.45 us: body(): lax.dot_general(bottom_in, bottom_grad, (((0,), (0,)), ((), ())), preferr...]
  transfers between devices with their start and end apart: 4 -> 12, of which waited for: 2 -> 4; matrix products, arithmetic and copies ran while one was open for 25% -> 2% of each run, Pallas kernels for 0% -> 15%
where the time goes in v1:
time: 231 us; the launch traced here: 230 us
  blocking collectives  109 us (47%)
  Pallas kernels  46.7 us (20%)
  starting transfers between devices  37.2 us (16%)
  waiting for transfers between devices  23.8 us (10%)
  local copies, waits for them, and re-layouts  5.46 us (2%)
  other arithmetic  3.77 us (2%)
  matrix products  3.26 us (1%)
    all_to_all x1, blocking collectives, exchange(): return lax.all_to_all(x, axis, split_axis=0, concat_axis=0, tiled=True)  109 us
    pallas_call x2, Pallas kernels, scattered(): pl.pallas_call(functools.partial(scatter_kernel, t), grid=(peers // PEERS...  25.4 us
    all_to_all x1, waiting for transfers between devices, body(): lax.all_to_all(copies, 'gx', split_axis=0, concat_axis=0, axis_index_grou...  17.5 us
    all_to_all x2, starting transfers between devices, exchange(): return lax.all_to_all(x, axis, split_axis=0, concat_axis=0, tiled=True)  14.5 us
    pallas_call x1, Pallas kernels, gathered(): pl.pallas_call(gather_kernel, grid_spec=pltpu.PrefetchScalarGridSpec(num_...  11.1 us
    pallas_call x1, Pallas kernels, slot_codes(): pl.pallas_call(slot_kernel, out_shape=jax.ShapeDtypeStruct((owners, table...  10.2 us
    all_to_all x1, starting transfers between devices, body(): lax.all_to_all(copies, 'gx', split_axis=0, concat_axis=0, axis_index_grou...  9 us
    ppermute x6, starting transfers between devices, passed(): lax.ppermute(give, 'gy', [(i, target(i, k)) for i in range(devices)])  8.74 us
  transfers between devices with their start and end apart: 12, of which 4 were waited for; matrix products, arithmetic and copies ran while one was open for 2% of the time, Pallas kernels for 15%

profile of v1, /device:TPU:1, one launch (start us, length us, event | category | flops | bytes accessed | tf_op | source)
XLA Modules:
  0.0 229.9 jit_solution(13942955859375174426)
XLA Ops:
  0.6 0.0 copy-start
  0.6 1.4 convert_reduce_fusion
  2.1 0.0 copy-start.1
  2.1 0.0 copy-start.2
  2.1 1.4 convolution_convert_fusion
  3.5 1.1 broadcast_in_dim.6
  4.6 9.0 %all-to-all-start.1 = ((bf16[8,2,128,256]{3,2,1,0:T(8,128)(2,1)}), bf16[8,2,128,256]{3,2,1,0:T(8,128)(2,1)}, u32[]{:S(2)}, u32[]{:S(2)}) async-start(bf16[8,2,128,256]{3,2,1,0:T(8,128)(2,1)} %broadcast_in_dim.6), calls=%async_computation.1 | async-start | bytes 2097152 | tf_op jit(solution)/shard_map/all_to_all | solution.py:258
  13.6 0.0 copy-done.1
  13.6 0.0 copy-done.2
  13.7 0.1 reshape.60
  13.8 0.0 copy-done
  13.8 1.5 convolution_bitcast_fusion
  15.2 0.1 copy.14
  15.3 0.1 reshape.59
  15.4 0.4 fusion.6
  15.8 0.1 select_maximum_fusion.1
  15.9 0.2 select_maximum_fusion
  16.1 0.1 constant_dynamic-slice_fusion
  16.2 1.0 collective-permute-start.1
  17.2 2.4 %collective-permute-done.1 = f32[16,16,1024]{2,1,0:T(8,128)} collective-permute-done((f32[16,16,1024]{2,1,0:T(8,128)S(1)}, f32[16,16,1024]{2,1,0:T(8,128)}, u32[]{:S(2)}, u32[]{:S(2)}) %collective-permute-start.1) | collective-permute-done | bytes 1048608 | tf_op jit(solution)/shard_map/ppermute | solution.py:291
  19.7 1.4 dynamic-slice_add_fusion
  21.0 0.1 dynamic-slice_bitcast_fusion.2
  21.1 1.3 collective-permute-start.2
  22.4 1.5 collective-permute-start.4
  23.9 1.5 collective-permute-start.3
  25.4 17.5 %all-to-all-done.1.mine_grad = bf16[8,2,128,256]{3,2,1,0:T(8,128)(2,1)} async-done(((bf16[8,2,128,256]{3,2,1,0:T(8,128)(2,1)}), bf16[8,2,128,256]{3,2,1,0:T(8,128)(2,1)}, u32[]{:S(2)}, u32[]{:S(2)}) %all-to-all-start.1) | async-done | bytes 1048608 | tf_op jit(solution)/shard_map/all_to_all | solution.py:258
  42.9 0.5 collective-permute-start
  43.4 10.2 %slots.1 = s32[256,128]{1,0:T(8,128)} custom-call(s32[2,32,256]{2,1,0:T(8,128)} %bitcast.55, s32[2,32,256]{2,1,0:T(8,128)} %bitcast.56), custom_call_target="tpu_custom_call" | custom-call | flops 4000000000 | bytes 262144 | tf_op jit(solution)/shard_map/slots/pallas_call | solution.py:70
  53.6 3.4 %all-to-all-start = ((s32[16,16,128]{2,1,0:T(8,128)}), s32[16,16,128]{2,1,0:T(8,128)S(1)}, u32[]{:S(2)}, u32[]{:S(2)}) async-start(s32[16,16,128]{2,1,0:T(8,128)} %bitcast.54), calls=%async_computation | async-start | bytes 262144 | tf_op jit(solution)/shard_map/all_to_all | solution.py:24
  57.2 0.0 collective-permute-done.2
  57.2 0.0 collective-permute-done.4
  57.2 0.0 collective-permute-done.3
  57.2 0.1 fusion.3
  57.3 1.4 collective-permute-start.5
  58.7 1.5 collective-permute-start.7
  60.2 1.6 collective-permute-start.6
  61.7 0.6 pad_add_fusion._
  62.3 0.0 collective-permute-done.5
  62.3 0.0 collective-permute-done.7
  62.3 2.8 %collective-permute-done.6 = f32[16,1024]{1,0:T(8,128)S(1)} collective-permute-done((f32[16,1024]{1,0:T(8,128)S(1)}, f32[16,1024]{1,0:T(8,128)S(1)}, u32[]{:S(2)}, u32[]{:S(2)}) %collective-permute-start.6) | collective-permute-done | bytes 65568 | tf_op jit(solution)/shard_map/ppermute | solution.py:229
  65.1 1.0 all-to-all-done.mine_ref.other_ref
  66.1 0.0 copy-start.3
  66.1 0.0 collective-permute-done.other_grad
  66.1 0.7 copy-done.3
  66.8 11.1 %gather.1 = bf16[16,272,1024]{2,1,0:T(8,128)(2,1)} custom-call(s32[2,8]{1,0:T(2,128)} %pad_add_fusion._, s32[16,16,128]{2,1,0:T(8,128)} %copy-done.3, s32[16,16,128]{2,1,0:T(8,128)} %copy-done.3, bf16[8,2,128,256]{3,2,1,0:T(8,128)(2,1)} %all-to-all-done.1.mine_grad, bf16[8,2,128,256]{3,2,1,0:T(8,128)(2,1)} %collective-permute-done.other_grad), custom_call_target="tpu_custom_call" | custom-call | flops 8000000000 | bytes 12582912 | tf_op jit(solution)/shard_map/gather/pallas_call | solution.py:133
  77.9 108.8 %all_to_all.25.refs_0_.refs_1_ = bf16[16,272,1024]{2,1,0:T(8,128)(2,1)} all-to-all(bf16[16,272,1024]{2,1,0:T(8,128)(2,1)} %gather.1), channel_id=1, replica_groups=mesh['gx'=16,'gy'=16] {'gy'}, dimensions={0} | all-to-all | bytes 17825792 | tf_op jit(solution)/shard_map/all_to_all | solution.py:24
  186.7 0.7 reshape.62
  187.4 3.4 %all-to-all-start.3 = ((f32[8,2,1024]{2,1,0:T(2,128)}), f32[8,2,1024]{2,1,0:T(2,128)S(1)}, u32[]{:S(2)}, u32[]{:S(2)}) async-start(f32[8,2,1024]{2,1,0:T(2,128)} %reshape.62), calls=%async_computation.3 | async-start | bytes 131072 | tf_op jit(solution)/shard_map/all_to_all | solution.py:300
  190.8 12.7 %scatter.2.refs_2_ = f32[2,2048,128]{2,1,0:T(8,128)} custom-call(bf16[16,272,1024]{2,1,0:T(8,128)(2,1)} %all_to_all.25.refs_0_.refs_1_, bf16[16,272,1024]{2,1,0:T(8,128)(2,1)} %all_to_all.25.refs_0_.refs_1_), custom_call_target="tpu_custom_call" | custom-call | flops 20000000000 | bytes 6291456 | tf_op jit(solution)/shard_map/scatter/pallas_call | solution.py:209
  203.5 0.0 all-to-all-done.3
  203.5 0.7 broadcast_in_dim.7
  204.2 11.1 %all-to-all-start.4 = ((f32[16,2,1024]{2,1,0:T(2,128)}), f32[16,2,1024]{2,1,0:T(2,128)S(1)}, u32[]{:S(2)}, u32[]{:S(2)}) async-start(f32[16,2,1024]{2,1,0:T(2,128)} %broadcast_in_dim.7), calls=%async_computation.4 | async-start | bytes 262144 | tf_op jit(solution)/shard_map/all_to_all | solution.py:24
  215.3 12.7 %scatter.3 = f32[2,2048,128]{2,1,0:T(8,128)} custom-call(bf16[16,272,1024]{2,1,0:T(8,128)(2,1)} %all_to_all.25.refs_0_.refs_1_, bf16[16,272,1024]{2,1,0:T(8,128)(2,1)} %all_to_all.25.refs_0_.refs_1_, f32[2,2048,128]{2,1,0:T(8,128)} %scatter.2.refs_2_), custom_call_target="tpu_custom_call", output_to_operand_aliasing={{}: (2, {})} | custom-call | flops 20000000000 | bytes 6291456 | tf_op jit(solution)/shard_map/scatter/pallas_call | solution.py:209
  228.0 0.0 all-to-all-done.4
  228.0 0.1 reshape.64
  228.1 0.5 slice_bitcast_fusion
  228.7 0.6 slice.20
  229.3 0.6 reshape.65
  (8 shorter events, 0.1 us)
Async XLA Ops:
  0.6 13.1 %copy-start = (bf16[256,256]{1,0:T(8,128)(2,1)S(1)}, bf16[256,256]{1,0:T(8,128)(2,1)}, u32[]{:S(2)}) copy-start(bf16[256,256]{1,0:T(8,128)(2,1)} %param.8) | copy-start | bytes 393220
  2.1 11.5 %copy-start.1 = (bf16[256,128]{1,0:T(8,128)(2,1)S(1)}, bf16[256,128]{1,0:T(8,128)(2,1)}, u32[]{:S(2)}) copy-start(bf16[256,128]{1,0:T(8,128)(2,1)} %param.9) | copy-start | bytes 196612
  2.1 11.5 %copy-start.2 = (bf16[256,2,128]{2,1,0:T(2,128)(2,1)S(1)}, bf16[256,2,128]{2,1,0:T(2,128)(2,1)}, u32[]{:S(2)}) copy-start(bf16[256,2,128]{2,1,0:T(2,128)(2,1)} %param.10) | copy-start | bytes 393220
  4.6 38.3 %all-to-all-start.1 = ((bf16[8,2,128,256]{3,2,1,0:T(8,128)(2,1)}), bf16[8,2,128,256]{3,2,1,0:T(8,128)(2,1)}, u32[]{:S(2)}, u32[]{:S(2)}) async-start(bf16[8,2,128,256]{3,2,1,0:T(8,128)(2,1)} %broadcast_in_dim.6), calls=%async_computation.1 | async-start | bytes 2097152 | tf_op jit(solution)/shard_map/all_to_all | solution.py:258
  16.2 3.5 %collective-permute-start.1 = (f32[16,16,1024]{2,1,0:T(8,128)S(1)}, f32[16,16,1024]{2,1,0:T(8,128)}, u32[]{:S(2)}, u32[]{:S(2)}) collective-permute-start(f32[16,16,1024]{2,1,0:T(8,128)S(1)} %constant_dynamic-slice_fusion), channel_id=1, source_target_pairs={{0,16},{16,0},{32,48},{48,32},{64,80},{80,64},{96,112},{112,96},{1... | collective-permute-start | bytes 3145736 | tf_op jit(solution)/shard_map/ppermute | solution.py:291
  21.1 36.1 %collective-permute-start.2 = (f32[4,16,1024]{2,1,0:T(8,128)S(1)}, f32[4,16,1024]{2,1,0:T(8,128)S(1)}, u32[]{:S(2)}, u32[]{:S(2)}) collective-permute-start(f32[4,16,1024]{2,1,0:T(8,128)S(1)} %get-tuple-element.14), channel_id=1, source_target_pairs={{0,1},{1,2},{2,3},{3,0},{4,5},{5,6},{6,7},{7,4},{8,9},{9,10},{10,1... | collective-permute-start | bytes 786440 | tf_op jit(solution)/shard_map/ppermute | solution.py:229
  22.4 34.8 %collective-permute-start.4 = (f32[4,16,1024]{2,1,0:T(8,128)S(1)}, f32[4,16,1024]{2,1,0:T(8,128)S(1)}, u32[]{:S(2)}, u32[]{:S(2)}) collective-permute-start(f32[4,16,1024]{2,1,0:T(8,128)S(1)} %get-tuple-element.15), channel_id=1, source_target_pairs={{0,3},{1,0},{2,1},{3,2},{4,7},{5,4},{6,5},{7,6},{8,11},{9,8},{10,9... | collective-permute-start | bytes 786440 | tf_op jit(solution)/shard_map/ppermute | solution.py:229
  23.9 33.3 %collective-permute-start.3 = (f32[4,16,1024]{2,1,0:T(8,128)S(1)}, f32[4,16,1024]{2,1,0:T(8,128)S(1)}, u32[]{:S(2)}, u32[]{:S(2)}) collective-permute-start(f32[4,16,1024]{2,1,0:T(8,128)S(1)} %get-tuple-element.16), channel_id=1, source_target_pairs={{0,2},{1,3},{2,0},{3,1},{4,6},{5,7},{6,4},{7,5},{8,10},{9,11},{10,... | collective-permute-start | bytes 786440 | tf_op jit(solution)/shard_map/ppermute | solution.py:229
  42.9 23.2 %collective-permute-start = (bf16[8,2,128,256]{3,2,1,0:T(8,128)(2,1)}, bf16[8,2,128,256]{3,2,1,0:T(8,128)(2,1)}, u32[]{:S(2)}, u32[]{:S(2)}) collective-permute-start(bf16[8,2,128,256]{3,2,1,0:T(8,128)(2,1)} %all-to-all-done.1.mine_grad), channel_id=1, source_target_pairs={{0,16},{16,0},{32,48},{48,32},{64,80},{80,64},{96,112},{112,96},{1... | collective-permute-start | bytes 3145736 | tf_op jit(solution)/shard_map/ppermute | solution.py:261
  53.6 12.5 %all-to-all-start = ((s32[16,16,128]{2,1,0:T(8,128)}), s32[16,16,128]{2,1,0:T(8,128)S(1)}, u32[]{:S(2)}, u32[]{:S(2)}) async-start(s32[16,16,128]{2,1,0:T(8,128)} %bitcast.54), calls=%async_computation | async-start | bytes 262144 | tf_op jit(solution)/shard_map/all_to_all | solution.py:24
  57.3 5.0 %collective-permute-start.5 = (f32[16,1024]{1,0:T(8,128)S(1)}, f32[16,1024]{1,0:T(8,128)S(1)}, u32[]{:S(2)}, u32[]{:S(2)}) collective-permute-start(f32[16,1024]{1,0:T(8,128)S(1)} %get-tuple-element.17), channel_id=1, source_target_pairs={{0,4},{1,5},{2,6},{3,7},{4,8},{5,9},{6,10},{7,11},{8,12},{9,13},{1... | collective-permute-start | bytes 196616 | tf_op jit(solution)/shard_map/ppermute | solution.py:229
  58.7 3.7 %collective-permute-start.7 = (f32[16,1024]{1,0:T(8,128)S(1)}, f32[16,1024]{1,0:T(8,128)S(1)}, u32[]{:S(2)}, u32[]{:S(2)}) collective-permute-start(f32[16,1024]{1,0:T(8,128)S(1)} %get-tuple-element.18), channel_id=1, source_target_pairs={{0,12},{1,13},{2,14},{3,15},{4,0},{5,1},{6,2},{7,3},{8,4},{9,5},{1... | collective-permute-start | bytes 196616 | tf_op jit(solution)/shard_map/ppermute | solution.py:229
  60.2 4.9 %collective-permute-start.6 = (f32[16,1024]{1,0:T(8,128)S(1)}, f32[16,1024]{1,0:T(8,128)S(1)}, u32[]{:S(2)}, u32[]{:S(2)}) collective-permute-start(f32[16,1024]{1,0:T(8,128)S(1)} %get-tuple-element.19), channel_id=1, source_target_pairs={{0,8},{1,9},{2,10},{3,11},{4,12},{5,13},{6,14},{7,15},{8,0},{9,1},... | collective-permute-start | bytes 196616 | tf_op jit(solution)/shard_map/ppermute | solution.py:229
  66.1 0.7 copy-start.3
  187.4 16.1 %all-to-all-start.3 = ((f32[8,2,1024]{2,1,0:T(2,128)}), f32[8,2,1024]{2,1,0:T(2,128)S(1)}, u32[]{:S(2)}, u32[]{:S(2)}) async-start(f32[8,2,1024]{2,1,0:T(2,128)} %reshape.62), calls=%async_computation.3 | async-start | bytes 131072 | tf_op jit(solution)/shard_map/all_to_all | solution.py:300
  204.2 23.8 %all-to-all-start.4 = ((f32[16,2,1024]{2,1,0:T(2,128)}), f32[16,2,1024]{2,1,0:T(2,128)S(1)}, u32[]{:S(2)}, u32[]{:S(2)}) async-start(f32[16,2,1024]{2,1,0:T(2,128)} %broadcast_in_dim.7), calls=%async_computation.4 | async-start | bytes 262144 | tf_op jit(solution)/shard_map/all_to_all | solution.py:24

commit v2 on v1

--- a/solution.py
+++ b/solution.py
@@ -13,7 +13,7 @@
 CORES = 2
 SIDE = 4
 GROUP = 8
-PEERS = 2
+PEERS = 4
 FREE = 256
 BAG_STEP = 4096
 NT = (((1,), (1,)), ((), ()))
@@ -75,7 +75,7 @@
             pltpu.VMEM((3 * CAP, lookups * bags), jnp.bfloat16),
         ],
         cost_estimate=pl.CostEstimate(
-            flops=4 * 10**9, bytes_accessed=262144, transcendentals=0
+            flops=10**6, bytes_accessed=262144, transcendentals=0
         ),
         name="slots",
     )(owner_lists, row_lists)
@@ -255,12 +255,12 @@
     grad = lax.dot_general(top_weight[width:], top_grad, NT, preferred_element_type=f32)
     grad = grad.astype(bf16).reshape(tables, width, bags)
     copies = jnp.broadcast_to(grad, (chips, tables, width, bags))
+    top_grad, bottom_in, bottom_pre, pooled, copies = lax.optimization_barrier(
+        (top_grad, bottom_in, bottom_pre, pooled, copies)
+    )
     mine = lax.all_to_all(
         copies, "gx", split_axis=0, concat_axis=0, axis_index_groups=columns, tiled=True
     )
-    other = lax.ppermute(mine, "gx", [(i, i ^ 1) for i in range(gx)])
-    payload = gathered(order, codes, mine, other)
-
     bottom_out = jnp.maximum(bottom_pre, jnp.zeros_like(bottom_pre))
     feature = jnp.concatenate([bottom_out, pooled.reshape(bags, tables * width)], axis=1)
     first = lax.dot_general(top_grad, top_weight[:width], NT, preferred_element_type=f32)
@@ -292,6 +292,9 @@
     part = part.reshape(gy // SIDE, SIDE, half, top)
     place = lax.axis_index("gy")
     part = passed(part, place % SIDE, 1, lambda i, k: i // SIDE * SIDE + (i + k) % SIDE, gy)
+    mine, part = lax.optimization_barrier((mine, part))
+    other = lax.ppermute(mine, "gx", [(i, i ^ 1) for i in range(gx)])
+    payload = gathered(order, codes, mine, other)
     part = passed(part, place // SIDE, 0, lambda i, k: (i + k * SIDE) % gy, gy)
     payload, part = lax.optimization_barrier((payload, part))
     arrived = exchange(payload, "gy")

time: 231 us -> 233 us (level)
  waiting for transfers between devices: 23.8 us -> 27.6 us
    ppermute x6, waiting for transfers between devices: 2.8 us -> 14.1 us  [passed(): lax.ppermute(give, 'gy', [(i, target(i, k)) for i in range(devices)])]
    all_to_all x1, waiting for transfers between devices: 17.5 us -> 12.3 us  [body(): lax.all_to_all(copies, 'gx', split_axis=0, concat_axis=0, axis_index_grou...]
    all_to_all x1, starting transfers between devices: 9 us -> 6.48 us  [body(): lax.all_to_all(copies, 'gx', split_axis=0, concat_axis=0, axis_index_grou...]
    ppermute x1, waiting for transfers between devices: 2.42 us -> 0.01 us  [body(): part = keep + lax.ppermute(give, 'gx', [(i, i ^ 1) for i in range(gx)])]
  transfers between devices with their start and end apart: 12 -> 12, of which waited for: 4 -> 5; matrix products, arithmetic and copies ran while one was open for 2% -> 1% of each run, Pallas kernels for 15% -> 15%
where the time goes in v2:
time: 233 us; the launch traced here: 232 us
  blocking collectives  109 us (47%)
  Pallas kernels  45.1 us (19%)
  starting transfers between devices  36.7 us (16%)
  waiting for transfers between devices  27.6 us (12%)
  local copies, waits for them, and re-layouts  6.34 us (3%)
  other arithmetic  3.72 us (2%)
  matrix products  3.24 us (1%)
    all_to_all x1, blocking collectives, exchange(): return lax.all_to_all(x, axis, split_axis=0, concat_axis=0, tiled=True)  109 us
    pallas_call x2, Pallas kernels, scattered(): pl.pallas_call(functools.partial(scatter_kernel, t), grid=(peers // PEERS...  23.8 us
    all_to_all x2, starting transfers between devices, exchange(): return lax.all_to_all(x, axis, split_axis=0, concat_axis=0, tiled=True)  14.4 us
    ppermute x6, waiting for transfers between devices, passed(): lax.ppermute(give, 'gy', [(i, target(i, k)) for i in range(devices)])  14.1 us
    all_to_all x1, waiting for transfers between devices, body(): lax.all_to_all(copies, 'gx', split_axis=0, concat_axis=0, axis_index_grou...  12.3 us
    pallas_call x1, Pallas kernels, gathered(): pl.pallas_call(gather_kernel, grid_spec=pltpu.PrefetchScalarGridSpec(num_...  11.1 us
    pallas_call x1, Pallas kernels, slot_codes(): pl.pallas_call(slot_kernel, out_shape=jax.ShapeDtypeStruct((owners, table...  10.2 us
    ppermute x6, starting transfers between devices, passed(): lax.ppermute(give, 'gy', [(i, target(i, k)) for i in range(devices)])  8.73 us
  transfers between devices with their start and end apart: 12, of which 5 were waited for; matrix products, arithmetic and copies ran while one was open for 1% of the time, Pallas kernels for 15%

profile of v2, /device:TPU:1, one launch (start us, length us, event | category | flops | bytes accessed | tf_op | source)
XLA Modules:
  0.0 232.5 jit_solution(3348197019031684661)
XLA Ops:
  0.6 0.0 copy-start
  0.7 0.0 copy-start.1
  0.7 0.0 copy-start.2
  0.7 1.3 compare_select_fusion
  2.0 1.4 convolution_convert_fusion
  3.4 1.1 broadcast_in_dim.6
  4.5 0.1 convert_reduce_fusion
  4.5 0.1 reshape.60
  4.6 0.0 copy-done.1
  4.6 0.0 copy-done.2
  4.7 0.0 copy-done
  4.7 1.5 fusion.1
  6.2 0.1 reshape.59
  6.2 0.1 select_maximum_fusion.1
  6.3 0.4 fusion.7
  6.7 0.2 select_maximum_fusion
  6.9 0.1 constant_dynamic-slice_fusion
  7.0 3.3 %collective-permute-start = (f32[16,16,1024]{2,1,0:T(8,128)S(1)}, f32[16,16,1024]{2,1,0:T(8,128)}, u32[]{:S(2)}, u32[]{:S(2)}) collective-permute-start(f32[16,16,1024]{2,1,0:T(8,128)S(1)} %constant_dynamic-slice_fusion), channel_id=1, source_target_pairs={{0,16},{16,0},{32,48},{48,32},{64,80},{80,64},{96,112},{112,96},{1... | collective-permute-start | bytes 3145736 | tf_op jit(solution)/shard_map/ppermute | solution.py:291
  10.3 6.5 %all-to-all-start.1 = ((bf16[8,2,128,256]{3,2,1,0:T(8,128)(2,1)}), bf16[8,2,128,256]{3,2,1,0:T(8,128)(2,1)}, u32[]{:S(2)}, u32[]{:S(2)}) async-start(bf16[8,2,128,256]{3,2,1,0:T(8,128)(2,1)} %broadcast_in_dim.6), calls=%async_computation.1 | async-start | bytes 2097152 | tf_op jit(solution)/shard_map/all_to_all | solution.py:261
  16.8 0.0 collective-permute-done
  16.8 1.4 dynamic-slice_add_fusion
  18.2 0.1 dynamic-slice_bitcast_fusion.2
  18.2 1.3 collective-permute-start.1
  19.5 1.5 collective-permute-start.3
  21.0 1.5 collective-permute-start.2
  22.5 4.7 %collective-permute-done.1 = f32[4,16,1024]{2,1,0:T(8,128)S(1)} collective-permute-done((f32[4,16,1024]{2,1,0:T(8,128)S(1)}, f32[4,16,1024]{2,1,0:T(8,128)S(1)}, u32[]{:S(2)}, u32[]{:S(2)}) %collective-permute-start.1) | collective-permute-done | bytes 262176 | tf_op jit(solution)/shard_map/ppermute | solution.py:229
  27.2 0.0 collective-permute-done.3
  27.2 6.6 %collective-permute-done.2 = f32[4,16,1024]{2,1,0:T(8,128)S(1)} collective-permute-done((f32[4,16,1024]{2,1,0:T(8,128)S(1)}, f32[4,16,1024]{2,1,0:T(8,128)S(1)}, u32[]{:S(2)}, u32[]{:S(2)}) %collective-permute-start.2) | collective-permute-done | bytes 262176 | tf_op jit(solution)/shard_map/ppermute | solution.py:229
  33.8 0.1 fusion.4
  33.9 12.3 %all-to-all-done.1.mine_grad = bf16[8,2,128,256]{3,2,1,0:T(8,128)(2,1)} async-done(((bf16[8,2,128,256]{3,2,1,0:T(8,128)(2,1)}), bf16[8,2,128,256]{3,2,1,0:T(8,128)(2,1)}, u32[]{:S(2)}, u32[]{:S(2)}) %all-to-all-start.1) | async-done | bytes 1048608 | tf_op jit(solution)/shard_map/all_to_all | solution.py:261
  46.2 0.5 collective-permute-start.4
  46.7 10.2 %slots.1 = s32[256,128]{1,0:T(8,128)} custom-call(s32[2,32,256]{2,1,0:T(8,128)} %bitcast.53, s32[2,32,256]{2,1,0:T(8,128)} %bitcast.54), custom_call_target="tpu_custom_call" | custom-call | flops 1000000 | bytes 262144 | tf_op jit(solution)/shard_map/slots/pallas_call | solution.py:70
  56.9 3.4 %all-to-all-start = ((s32[16,16,128]{2,1,0:T(8,128)}), s32[16,16,128]{2,1,0:T(8,128)S(1)}, u32[]{:S(2)}, u32[]{:S(2)}) async-start(s32[16,16,128]{2,1,0:T(8,128)} %bitcast.49), calls=%async_computation | async-start | bytes 262144 | tf_op jit(solution)/shard_map/all_to_all | solution.py:24
  60.4 1.4 collective-permute-start.5
  61.8 1.5 collective-permute-start.7
  63.3 1.6 collective-permute-start.6
  64.9 0.6 pad_add_fusion._
  65.5 0.0 collective-permute-done.5
  65.5 0.0 collective-permute-done.7
  65.5 2.8 %collective-permute-done.6 = f32[16,1024]{1,0:T(8,128)S(1)} collective-permute-done((f32[16,1024]{1,0:T(8,128)S(1)}, f32[16,1024]{1,0:T(8,128)S(1)}, u32[]{:S(2)}, u32[]{:S(2)}) %collective-permute-start.6) | collective-permute-done | bytes 65568 | tf_op jit(solution)/shard_map/ppermute | solution.py:229
  68.3 1.2 all-to-all-done.mine_ref.other_ref
  69.4 0.0 copy-start.3
  69.4 0.0 collective-permute-done.4.other_grad
  69.4 0.6 copy-done.3
  70.1 0.0 copy-start.4
  70.1 1.0 copy-done.4
  71.0 11.1 %gather.1 = bf16[16,272,1024]{2,1,0:T(8,128)(2,1)} custom-call(s32[2,8]{1,0:T(2,128)} %pad_add_fusion._, s32[16,16,128]{2,1,0:T(8,128)} %copy-done.3, s32[16,16,128]{2,1,0:T(8,128)} %copy-done.3, bf16[8,2,128,256]{3,2,1,0:T(8,128)(2,1)} %all-to-all-done.1.mine_grad, bf16[8,2,128,256]{3,2,1,0:T(8,128)(2,1)} %copy-done.4), custom_call_target="tpu_custom_call" | custom-call | flops 8000000000 | bytes 12582912 | tf_op jit(solution)/shard_map/gather/pallas_call | solution.py:133
  82.1 108.8 %all_to_all.25.refs_0_.refs_1_ = bf16[16,272,1024]{2,1,0:T(8,128)(2,1)} all-to-all(bf16[16,272,1024]{2,1,0:T(8,128)(2,1)} %gather.1), channel_id=1, replica_groups=mesh['gx'=16,'gy'=16] {'gy'}, dimensions={0} | all-to-all | bytes 17825792 | tf_op jit(solution)/shard_map/all_to_all | solution.py:24
  191.0 0.7 reshape.62
  191.7 3.4 %all-to-all-start.3 = ((f32[8,2,1024]{2,1,0:T(2,128)}), f32[8,2,1024]{2,1,0:T(2,128)S(1)}, u32[]{:S(2)}, u32[]{:S(2)}) async-start(f32[8,2,1024]{2,1,0:T(2,128)} %reshape.62), calls=%async_computation.3 | async-start | bytes 131072 | tf_op jit(solution)/shard_map/all_to_all | solution.py:303
  195.0 11.9 %scatter.2.refs_2_ = f32[2,2048,128]{2,1,0:T(8,128)} custom-call(bf16[16,272,1024]{2,1,0:T(8,128)(2,1)} %all_to_all.25.refs_0_.refs_1_, bf16[16,272,1024]{2,1,0:T(8,128)(2,1)} %all_to_all.25.refs_0_.refs_1_), custom_call_target="tpu_custom_call" | custom-call | flops 20000000000 | bytes 6291456 | tf_op jit(solution)/shard_map/scatter/pallas_call | solution.py:209
  206.9 0.0 all-to-all-done.3
  207.0 0.7 broadcast_in_dim.7
  207.7 11.0 %all-to-all-start.4 = ((f32[16,2,1024]{2,1,0:T(2,128)}), f32[16,2,1024]{2,1,0:T(2,128)S(1)}, u32[]{:S(2)}, u32[]{:S(2)}) async-start(f32[16,2,1024]{2,1,0:T(2,128)} %broadcast_in_dim.7), calls=%async_computation.4 | async-start | bytes 262144 | tf_op jit(solution)/shard_map/all_to_all | solution.py:24
  218.7 11.9 %scatter.3 = f32[2,2048,128]{2,1,0:T(8,128)} custom-call(bf16[16,272,1024]{2,1,0:T(8,128)(2,1)} %all_to_all.25.refs_0_.refs_1_, bf16[16,272,1024]{2,1,0:T(8,128)(2,1)} %all_to_all.25.refs_0_.refs_1_, f32[2,2048,128]{2,1,0:T(8,128)} %scatter.2.refs_2_), custom_call_target="tpu_custom_call", output_to_operand_aliasing={{}: (2, {})} | custom-call | flops 20000000000 | bytes 6291456 | tf_op jit(solution)/shard_map/scatter/pallas_call | solution.py:209
  230.6 0.0 all-to-all-done.4
  230.6 0.1 reshape.64
  230.7 0.5 slice_bitcast_fusion
  231.2 0.6 slice.20
  231.8 0.6 reshape.65
  (8 shorter events, 0.1 us)
Async XLA Ops:
  0.6 4.0 %copy-start = (bf16[256,256]{1,0:T(8,128)(2,1)S(1)}, bf16[256,256]{1,0:T(8,128)(2,1)}, u32[]{:S(2)}) copy-start(bf16[256,256]{1,0:T(8,128)(2,1)} %param.8) | copy-start | bytes 393220
  0.7 4.0 %copy-start.1 = (bf16[256,128]{1,0:T(8,128)(2,1)S(1)}, bf16[256,128]{1,0:T(8,128)(2,1)}, u32[]{:S(2)}) copy-start(bf16[256,128]{1,0:T(8,128)(2,1)} %param.9) | copy-start | bytes 196612
  0.7 4.0 %copy-start.2 = (bf16[256,2,128]{2,1,0:T(2,128)(2,1)S(1)}, bf16[256,2,128]{2,1,0:T(2,128)(2,1)}, u32[]{:S(2)}) copy-start(bf16[256,2,128]{2,1,0:T(2,128)(2,1)} %param.10) | copy-start | bytes 393220
  7.0 9.8 %collective-permute-start = (f32[16,16,1024]{2,1,0:T(8,128)S(1)}, f32[16,16,1024]{2,1,0:T(8,128)}, u32[]{:S(2)}, u32[]{:S(2)}) collective-permute-start(f32[16,16,1024]{2,1,0:T(8,128)S(1)} %constant_dynamic-slice_fusion), channel_id=1, source_target_pairs={{0,16},{16,0},{32,48},{48,32},{64,80},{80,64},{96,112},{112,96},{1... | collective-permute-start | bytes 3145736 | tf_op jit(solution)/shard_map/ppermute | solution.py:291
  10.3 35.9 %all-to-all-start.1 = ((bf16[8,2,128,256]{3,2,1,0:T(8,128)(2,1)}), bf16[8,2,128,256]{3,2,1,0:T(8,128)(2,1)}, u32[]{:S(2)}, u32[]{:S(2)}) async-start(bf16[8,2,128,256]{3,2,1,0:T(8,128)(2,1)} %broadcast_in_dim.6), calls=%async_computation.1 | async-start | bytes 2097152 | tf_op jit(solution)/shard_map/all_to_all | solution.py:261
  18.2 9.0 %collective-permute-start.1 = (f32[4,16,1024]{2,1,0:T(8,128)S(1)}, f32[4,16,1024]{2,1,0:T(8,128)S(1)}, u32[]{:S(2)}, u32[]{:S(2)}) collective-permute-start(f32[4,16,1024]{2,1,0:T(8,128)S(1)} %get-tuple-element.26), channel_id=1, source_target_pairs={{0,1},{1,2},{2,3},{3,0},{4,5},{5,6},{6,7},{7,4},{8,9},{9,10},{10,1... | collective-permute-start | bytes 786440 | tf_op jit(solution)/shard_map/ppermute | solution.py:229
  19.5 7.7 %collective-permute-start.3 = (f32[4,16,1024]{2,1,0:T(8,128)S(1)}, f32[4,16,1024]{2,1,0:T(8,128)S(1)}, u32[]{:S(2)}, u32[]{:S(2)}) collective-permute-start(f32[4,16,1024]{2,1,0:T(8,128)S(1)} %get-tuple-element.27), channel_id=1, source_target_pairs={{0,3},{1,0},{2,1},{3,2},{4,7},{5,4},{6,5},{7,6},{8,11},{9,8},{10,9... | collective-permute-start | bytes 786440 | tf_op jit(solution)/shard_map/ppermute | solution.py:229
  21.0 12.8 %collective-permute-start.2 = (f32[4,16,1024]{2,1,0:T(8,128)S(1)}, f32[4,16,1024]{2,1,0:T(8,128)S(1)}, u32[]{:S(2)}, u32[]{:S(2)}) collective-permute-start(f32[4,16,1024]{2,1,0:T(8,128)S(1)} %get-tuple-element.28), channel_id=1, source_target_pairs={{0,2},{1,3},{2,0},{3,1},{4,6},{5,7},{6,4},{7,5},{8,10},{9,11},{10,... | collective-permute-start | bytes 786440 | tf_op jit(solution)/shard_map/ppermute | solution.py:229
  46.2 23.2 %collective-permute-start.4 = (bf16[8,2,128,256]{3,2,1,0:T(8,128)(2,1)}, bf16[8,2,128,256]{3,2,1,0:T(8,128)(2,1)S(1)}, u32[]{:S(2)}, u32[]{:S(2)}) collective-permute-start(bf16[8,2,128,256]{3,2,1,0:T(8,128)(2,1)} %all-to-all-done.1.mine_grad), channel_id=1, source_target_pairs={{0,16},{16,0},{32,48},{48,32},{64,80},{80,64},{96,112},{112,96},{1... | collective-permute-start | bytes 3145736 | tf_op jit(solution)/shard_map/ppermute | solution.py:296
  56.9 12.5 %all-to-all-start = ((s32[16,16,128]{2,1,0:T(8,128)}), s32[16,16,128]{2,1,0:T(8,128)S(1)}, u32[]{:S(2)}, u32[]{:S(2)}) async-start(s32[16,16,128]{2,1,0:T(8,128)} %bitcast.49), calls=%async_computation | async-start | bytes 262144 | tf_op jit(solution)/shard_map/all_to_all | solution.py:24
  60.4 5.0 %collective-permute-start.5 = (f32[16,1024]{1,0:T(8,128)S(1)}, f32[16,1024]{1,0:T(8,128)S(1)}, u32[]{:S(2)}, u32[]{:S(2)}) collective-permute-start(f32[16,1024]{1,0:T(8,128)S(1)} %get-tuple-element.29), channel_id=1, source_target_pairs={{0,4},{1,5},{2,6},{3,7},{4,8},{5,9},{6,10},{7,11},{8,12},{9,13},{1... | collective-permute-start | bytes 196616 | tf_op jit(solution)/shard_map/ppermute | solution.py:229
  61.8 3.7 %collective-permute-start.7 = (f32[16,1024]{1,0:T(8,128)S(1)}, f32[16,1024]{1,0:T(8,128)S(1)}, u32[]{:S(2)}, u32[]{:S(2)}) collective-permute-start(f32[16,1024]{1,0:T(8,128)S(1)} %get-tuple-element.30), channel_id=1, source_target_pairs={{0,12},{1,13},{2,14},{3,15},{4,0},{5,1},{6,2},{7,3},{8,4},{9,5},{1... | collective-permute-start | bytes 196616 | tf_op jit(solution)/shard_map/ppermute | solution.py:229
  63.3 4.9 %collective-permute-start.6 = (f32[16,1024]{1,0:T(8,128)S(1)}, f32[16,1024]{1,0:T(8,128)S(1)}, u32[]{:S(2)}, u32[]{:S(2)}) collective-permute-start(f32[16,1024]{1,0:T(8,128)S(1)} %get-tuple-element.31), channel_id=1, source_target_pairs={{0,8},{1,9},{2,10},{3,11},{4,12},{5,13},{6,14},{7,15},{8,0},{9,1},... | collective-permute-start | bytes 196616 | tf_op jit(solution)/shard_map/ppermute | solution.py:229
  69.4 0.7 copy-start.3
  70.1 1.0 copy-start.4
  191.7 15.3 %all-to-all-start.3 = ((f32[8,2,1024]{2,1,0:T(2,128)}), f32[8,2,1024]{2,1,0:T(2,128)S(1)}, u32[]{:S(2)}, u32[]{:S(2)}) async-start(f32[8,2,1024]{2,1,0:T(2,128)} %reshape.62), calls=%async_computation.3 | async-start | bytes 131072 | tf_op jit(solution)/shard_map/all_to_all | solution.py:303
  207.7 22.9 %all-to-all-start.4 = ((f32[16,2,1024]{2,1,0:T(2,128)}), f32[16,2,1024]{2,1,0:T(2,128)S(1)}, u32[]{:S(2)}, u32[]{:S(2)}) async-start(f32[16,2,1024]{2,1,0:T(2,128)} %broadcast_in_dim.7), calls=%async_computation.4 | async-start | bytes 262144 | tf_op jit(solution)/shard_map/all_to_all | solution.py:24

commit v3 on v2

--- a/solution.py
+++ b/solution.py
@@ -296,17 +296,17 @@
     other = lax.ppermute(mine, "gx", [(i, i ^ 1) for i in range(gx)])
     payload = gathered(order, codes, mine, other)
     part = passed(part, place // SIDE, 0, lambda i, k: (i + k * SIDE) % gy, gy)
-    payload, part = lax.optimization_barrier((payload, part))
+    copies = jnp.broadcast_to(part, (chips, half, top))
+    payload, copies = lax.optimization_barrier((payload, copies))
     arrived = exchange(payload, "gy")
-    part, arrived = lax.optimization_barrier((part, arrived))
-
+    copies, arrived = lax.optimization_barrier((copies, arrived))
     part = lax.all_to_all(
-        part.reshape(chips, half // chips, top),
-        "gx", split_axis=0, concat_axis=0, axis_index_groups=columns, tiled=True,
+        copies, "gx", split_axis=0, concat_axis=0, axis_index_groups=columns, tiled=True
     )
     part = jnp.sum(part, axis=0)
-    total = exchange(jnp.broadcast_to(part, (gx, *part.shape)), "gx")
-    total = total.reshape(chips, CORES, *part.shape).transpose(1, 0, 2, 3).reshape(-1, top)
+    twin = lax.ppermute(part, "gx", [(i, i ^ 1) for i in range(gx)])
+    even = (me & 1) == 0
+    total = jnp.concatenate([jnp.where(even, part, twin), jnp.where(even, twin, part)], axis=0)
     top_weight_grad = total[:top_rows]
     bottom_weight_grad = total[top_rows : top_rows + bottom_rows].reshape(-1, width)
     top_bias_grad = total[top_rows + bottom_rows, : top // gy]

time: 233 us -> 262 us (1.12)
  waiting for transfers between devices: 27.6 us -> 169 us
  blocking collectives: 109 us -> 0 us
  starting transfers between devices: 36.7 us -> 33.5 us
    all_to_all x2, waiting for transfers between devices: 1.16 us -> 137 us  [exchange(): return lax.all_to_all(x, axis, split_axis=0, concat_axis=0, tiled=True)]
    all_to_all x1 -> x0, blocking collectives: 109 us -> none  [exchange(): return lax.all_to_all(x, axis, split_axis=0, concat_axis=0, tiled=True)]
    all_to_all x1 -> x2, waiting for transfers between devices: 12.3 us -> 18.3 us  [body(): lax.all_to_all(copies, 'gx', split_axis=0, concat_axis=0, axis_index_grou...]
    all_to_all x2, starting transfers between devices: 14.4 us -> 10.4 us  [exchange(): return lax.all_to_all(x, axis, split_axis=0, concat_axis=0, tiled=True)]
    all_to_all x1 -> x2, starting transfers between devices: 6.48 us -> 9.98 us  [body(): lax.all_to_all(copies, 'gx', split_axis=0, concat_axis=0, axis_index_grou...]
    all_to_all x1 -> x0, starting transfers between devices: 3.35 us -> none  [body(): lax.all_to_all(part.reshape(chips, half // chips, top), 'gx', split_axis=...]
  transfers between devices with their start and end apart: 12 -> 13, of which waited for: 5 -> 7; matrix products, arithmetic and copies ran while one was open for 1% -> 1% of each run, Pallas kernels for 15% -> 13%
where the time goes in v3:
time: 262 us
  waiting for transfers between devices  169 us (65%)
  Pallas kernels  45.1 us (17%)
  starting transfers between devices  33.5 us (13%)
  local copies, waits for them, and re-layouts  5.08 us (2%)
  other arithmetic  4.37 us (2%)
  matrix products  3.24 us (1%)
    all_to_all x2, waiting for transfers between devices, exchange(): return lax.all_to_all(x, axis, split_axis=0, concat_axis=0, tiled=True)  137 us
    pallas_call x2, Pallas kernels, scattered(): pl.pallas_call(functools.partial(scatter_kernel, t), grid=(peers // PEERS...  23.8 us
    all_to_all x2, waiting for transfers between devices, body(): lax.all_to_all(copies, 'gx', split_axis=0, concat_axis=0, axis_index_grou...  18.3 us
    ppermute x6, waiting for transfers between devices, passed(): lax.ppermute(give, 'gy', [(i, target(i, k)) for i in range(devices)])  14.1 us
    pallas_call x1, Pallas kernels, gathered(): pl.pallas_call(gather_kernel, grid_spec=pltpu.PrefetchScalarGridSpec(num_...  11.1 us
    all_to_all x2, starting transfers between devices, exchange(): return lax.all_to_all(x, axis, split_axis=0, concat_axis=0, tiled=True)  10.4 us
    pallas_call x1, Pallas kernels, slot_codes(): pl.pallas_call(slot_kernel, out_shape=jax.ShapeDtypeStruct((owners, table...  10.2 us
    all_to_all x2, starting transfers between devices, body(): lax.all_to_all(copies, 'gx', split_axis=0, concat_axis=0, axis_index_grou...  9.98 us
  transfers between devices with their start and end apart: 13, of which 7 were waited for; matrix products, arithmetic and copies ran while one was open for 1% of the time, Pallas kernels for 13%

profile of v3, /device:TPU:1, one launch (start us, length us, event | category | flops | bytes accessed | tf_op | source)
XLA Modules:
  0.0 261.5 jit_solution(10119581864832221484)
XLA Ops:
  0.6 0.0 copy-start
  0.7 0.0 copy-start.1
  0.7 0.0 copy-start.2
  0.7 1.3 compare_select_fusion
  2.0 1.4 convolution_convert_fusion
  3.4 1.1 broadcast_in_dim.6
  4.5 0.1 convert_reduce_fusion
  4.5 0.1 reshape.51
  4.6 0.0 copy-done.1
  4.6 0.0 copy-done.2
  4.7 0.0 copy-done
  4.7 1.5 fusion.1
  6.2 0.1 reshape.50
  6.2 0.1 select_maximum_fusion.1
  6.3 0.4 fusion.7
  6.7 0.2 select_maximum_fusion
  6.9 0.1 constant_dynamic-slice_fusion
  7.0 3.3 %collective-permute-start = (f32[16,16,1024]{2,1,0:T(8,128)S(1)}, f32[16,16,1024]{2,1,0:T(8,128)}, u32[]{:S(2)}, u32[]{:S(2)}) collective-permute-start(f32[16,16,1024]{2,1,0:T(8,128)S(1)} %constant_dynamic-slice_fusion), channel_id=1, source_target_pairs={{0,16},{16,0},{32,48},{48,32},{64,80},{80,64},{96,112},{112,96},{1... | collective-permute-start | bytes 3145736 | tf_op jit(solution)/shard_map/ppermute | solution.py:291
  10.3 6.5 %all-to-all-start.1 = ((bf16[8,2,128,256]{3,2,1,0:T(8,128)(2,1)}), bf16[8,2,128,256]{3,2,1,0:T(8,128)(2,1)}, u32[]{:S(2)}, u32[]{:S(2)}) async-start(bf16[8,2,128,256]{3,2,1,0:T(8,128)(2,1)} %broadcast_in_dim.6), calls=%async_computation.1 | async-start | bytes 2097152 | tf_op jit(solution)/shard_map/all_to_all | solution.py:261
  16.8 0.0 collective-permute-done
  16.8 1.4 dynamic-slice_add_fusion
  18.2 0.1 dynamic-slice_bitcast_fusion.2
  18.2 1.3 collective-permute-start.1
  19.5 1.5 collective-permute-start.3
  21.0 1.5 collective-permute-start.2
  22.5 4.7 %collective-permute-done.1 = f32[4,16,1024]{2,1,0:T(8,128)S(1)} collective-permute-done((f32[4,16,1024]{2,1,0:T(8,128)S(1)}, f32[4,16,1024]{2,1,0:T(8,128)S(1)}, u32[]{:S(2)}, u32[]{:S(2)}) %collective-permute-start.1) | collective-permute-done | bytes 262176 | tf_op jit(solution)/shard_map/ppermute | solution.py:229
  27.2 0.0 collective-permute-done.3
  27.2 6.6 %collective-permute-done.2 = f32[4,16,1024]{2,1,0:T(8,128)S(1)} collective-permute-done((f32[4,16,1024]{2,1,0:T(8,128)S(1)}, f32[4,16,1024]{2,1,0:T(8,128)S(1)}, u32[]{:S(2)}, u32[]{:S(2)}) %collective-permute-start.2) | collective-permute-done | bytes 262176 | tf_op jit(solution)/shard_map/ppermute | solution.py:229
  33.8 0.1 fusion.4
  33.9 12.3 %all-to-all-done.1.mine_grad = bf16[8,2,128,256]{3,2,1,0:T(8,128)(2,1)} async-done(((bf16[8,2,128,256]{3,2,1,0:T(8,128)(2,1)}), bf16[8,2,128,256]{3,2,1,0:T(8,128)(2,1)}, u32[]{:S(2)}, u32[]{:S(2)}) %all-to-all-start.1) | async-done | bytes 1048608 | tf_op jit(solution)/shard_map/all_to_all | solution.py:261
  46.2 0.5 collective-permute-start.4
  46.7 10.2 %slots.1 = s32[256,128]{1,0:T(8,128)} custom-call(s32[2,32,256]{2,1,0:T(8,128)} %bitcast.49, s32[2,32,256]{2,1,0:T(8,128)} %bitcast.50), custom_call_target="tpu_custom_call" | custom-call | flops 1000000 | bytes 262144 | tf_op jit(solution)/shard_map/slots/pallas_call | solution.py:70
  56.9 3.4 %all-to-all-start = ((s32[16,16,128]{2,1,0:T(8,128)}), s32[16,16,128]{2,1,0:T(8,128)S(1)}, u32[]{:S(2)}, u32[]{:S(2)}) async-start(s32[16,16,128]{2,1,0:T(8,128)} %bitcast.46), calls=%async_computation | async-start | bytes 262144 | tf_op jit(solution)/shard_map/all_to_all | solution.py:24
  60.4 1.4 collective-permute-start.5
  61.8 1.5 collective-permute-start.7
  63.3 1.6 collective-permute-start.6
  64.9 0.6 pad_add_fusion._
  65.5 0.0 collective-permute-done.5
  65.5 0.0 collective-permute-done.7
  65.5 2.8 %collective-permute-done.6 = f32[16,1024]{1,0:T(8,128)S(1)} collective-permute-done((f32[16,1024]{1,0:T(8,128)S(1)}, f32[16,1024]{1,0:T(8,128)S(1)}, u32[]{:S(2)}, u32[]{:S(2)}) %collective-permute-start.6) | collective-permute-done | bytes 65568 | tf_op jit(solution)/shard_map/ppermute | solution.py:229
  68.3 1.2 all-to-all-done.mine_ref.other_ref
  69.4 0.0 copy-start.3
  69.4 0.0 collective-permute-done.4.other_grad
  69.4 0.6 copy-done.3
  70.1 0.0 copy-start.4
  70.1 1.0 copy-done.4
  71.0 11.1 %gather.1 = bf16[16,272,1024]{2,1,0:T(8,128)(2,1)} custom-call(s32[2,8]{1,0:T(2,128)} %pad_add_fusion._, s32[16,16,128]{2,1,0:T(8,128)} %copy-done.3, s32[16,16,128]{2,1,0:T(8,128)} %copy-done.3, bf16[8,2,128,256]{3,2,1,0:T(8,128)(2,1)} %all-to-all-done.1.mine_grad, bf16[8,2,128,256]{3,2,1,0:T(8,128)(2,1)} %copy-done.4), custom_call_target="tpu_custom_call" | custom-call | flops 8000000000 | bytes 12582912 | tf_op jit(solution)/shard_map/gather/pallas_call | solution.py:133
  82.1 0.9 broadcast_in_dim.7
  83.0 7.0 %all-to-all-start.2 = ((bf16[16,272,1024]{2,1,0:T(8,128)(2,1)}), bf16[16,272,1024]{2,1,0:T(8,128)(2,1)}, u32[]{:S(2)}, u32[]{:S(2)}) async-start(bf16[16,272,1024]{2,1,0:T(8,128)(2,1)} %gather.1), calls=%async_computation.2 | async-start | bytes 17825792 | tf_op jit(solution)/shard_map/all_to_all | solution.py:24
  90.0 135.8 %all-to-all-done.2.refs_0_.refs_1_ = bf16[16,272,1024]{2,1,0:T(8,128)(2,1)} async-done(((bf16[16,272,1024]{2,1,0:T(8,128)(2,1)}), bf16[16,272,1024]{2,1,0:T(8,128)(2,1)}, u32[]{:S(2)}, u32[]{:S(2)}) %all-to-all-start.2) | async-done | bytes 8912928 | tf_op jit(solution)/shard_map/all_to_all | solution.py:24
  225.9 3.5 %all-to-all-start.3 = ((f32[8,16,1024]{2,1,0:T(8,128)}), f32[8,16,1024]{2,1,0:T(8,128)S(1)}, u32[]{:S(2)}, u32[]{:S(2)}) async-start(f32[8,16,1024]{2,1,0:T(8,128)} %broadcast_in_dim.7), calls=%async_computation.3 | async-start | bytes 1048576 | tf_op jit(solution)/shard_map/all_to_all | solution.py:303
  229.4 11.9 %scatter.2.refs_2_ = f32[2,2048,128]{2,1,0:T(8,128)} custom-call(bf16[16,272,1024]{2,1,0:T(8,128)(2,1)} %all-to-all-done.2.refs_0_.refs_1_, bf16[16,272,1024]{2,1,0:T(8,128)(2,1)} %all-to-all-done.2.refs_0_.refs_1_), custom_call_target="tpu_custom_call" | custom-call | flops 20000000000 | bytes 6291456 | tf_op jit(solution)/shard_map/scatter/pallas_call | solution.py:209
  241.3 6.0 %all-to-all-done.3 = f32[8,16,1024]{2,1,0:T(8,128)S(1)} async-done(((f32[8,16,1024]{2,1,0:T(8,128)}), f32[8,16,1024]{2,1,0:T(8,128)S(1)}, u32[]{:S(2)}, u32[]{:S(2)}) %all-to-all-start.3) | async-done | bytes 524320 | tf_op jit(solution)/shard_map/all_to_all | solution.py:303
  247.3 0.6 collective-permute-start.8
  247.9 11.9 %scatter.3 = f32[2,2048,128]{2,1,0:T(8,128)} custom-call(bf16[16,272,1024]{2,1,0:T(8,128)(2,1)} %all-to-all-done.2.refs_0_.refs_1_, bf16[16,272,1024]{2,1,0:T(8,128)(2,1)} %all-to-all-done.2.refs_0_.refs_1_, f32[2,2048,128]{2,1,0:T(8,128)} %scatter.2.refs_2_), custom_call_target="tpu_custom_call", output_to_operand_aliasing={{}: (2, {})} | custom-call | flops 20000000000 | bytes 6291456 | tf_op jit(solution)/shard_map/scatter/pallas_call | solution.py:209
  259.8 0.0 collective-permute-done.8
  259.8 0.5 slice_bitcast_fusion
  260.3 0.6 pad_maximum_fusion
  260.9 0.6 reshape.53
  (8 shorter events, 0.1 us)
Async XLA Ops:
  0.6 4.0 %copy-start = (bf16[256,256]{1,0:T(8,128)(2,1)S(1)}, bf16[256,256]{1,0:T(8,128)(2,1)}, u32[]{:S(2)}) copy-start(bf16[256,256]{1,0:T(8,128)(2,1)} %param.8) | copy-start | bytes 393220
  0.7 4.0 %copy-start.1 = (bf16[256,128]{1,0:T(8,128)(2,1)S(1)}, bf16[256,128]{1,0:T(8,128)(2,1)}, u32[]{:S(2)}) copy-start(bf16[256,128]{1,0:T(8,128)(2,1)} %param.9) | copy-start | bytes 196612
  0.7 4.0 %copy-start.2 = (bf16[256,2,128]{2,1,0:T(2,128)(2,1)S(1)}, bf16[256,2,128]{2,1,0:T(2,128)(2,1)}, u32[]{:S(2)}) copy-start(bf16[256,2,128]{2,1,0:T(2,128)(2,1)} %param.10) | copy-start | bytes 393220
  7.0 9.8 %collective-permute-start = (f32[16,16,1024]{2,1,0:T(8,128)S(1)}, f32[16,16,1024]{2,1,0:T(8,128)}, u32[]{:S(2)}, u32[]{:S(2)}) collective-permute-start(f32[16,16,1024]{2,1,0:T(8,128)S(1)} %constant_dynamic-slice_fusion), channel_id=1, source_target_pairs={{0,16},{16,0},{32,48},{48,32},{64,80},{80,64},{96,112},{112,96},{1... | collective-permute-start | bytes 3145736 | tf_op jit(solution)/shard_map/ppermute | solution.py:291
  10.3 35.9 %all-to-all-start.1 = ((bf16[8,2,128,256]{3,2,1,0:T(8,128)(2,1)}), bf16[8,2,128,256]{3,2,1,0:T(8,128)(2,1)}, u32[]{:S(2)}, u32[]{:S(2)}) async-start(bf16[8,2,128,256]{3,2,1,0:T(8,128)(2,1)} %broadcast_in_dim.6), calls=%async_computation.1 | async-start | bytes 2097152 | tf_op jit(solution)/shard_map/all_to_all | solution.py:261
  18.2 9.0 %collective-permute-start.1 = (f32[4,16,1024]{2,1,0:T(8,128)S(1)}, f32[4,16,1024]{2,1,0:T(8,128)S(1)}, u32[]{:S(2)}, u32[]{:S(2)}) collective-permute-start(f32[4,16,1024]{2,1,0:T(8,128)S(1)} %get-tuple-element.26), channel_id=1, source_target_pairs={{0,1},{1,2},{2,3},{3,0},{4,5},{5,6},{6,7},{7,4},{8,9},{9,10},{10,1... | collective-permute-start | bytes 786440 | tf_op jit(solution)/shard_map/ppermute | solution.py:229
  19.5 7.7 %collective-permute-start.3 = (f32[4,16,1024]{2,1,0:T(8,128)S(1)}, f32[4,16,1024]{2,1,0:T(8,128)S(1)}, u32[]{:S(2)}, u32[]{:S(2)}) collective-permute-start(f32[4,16,1024]{2,1,0:T(8,128)S(1)} %get-tuple-element.27), channel_id=1, source_target_pairs={{0,3},{1,0},{2,1},{3,2},{4,7},{5,4},{6,5},{7,6},{8,11},{9,8},{10,9... | collective-permute-start | bytes 786440 | tf_op jit(solution)/shard_map/ppermute | solution.py:229
  21.0 12.8 %collective-permute-start.2 = (f32[4,16,1024]{2,1,0:T(8,128)S(1)}, f32[4,16,1024]{2,1,0:T(8,128)S(1)}, u32[]{:S(2)}, u32[]{:S(2)}) collective-permute-start(f32[4,16,1024]{2,1,0:T(8,128)S(1)} %get-tuple-element.28), channel_id=1, source_target_pairs={{0,2},{1,3},{2,0},{3,1},{4,6},{5,7},{6,4},{7,5},{8,10},{9,11},{10,... | collective-permute-start | bytes 786440 | tf_op jit(solution)/shard_map/ppermute | solution.py:229
  46.2 23.2 %collective-permute-start.4 = (bf16[8,2,128,256]{3,2,1,0:T(8,128)(2,1)}, bf16[8,2,128,256]{3,2,1,0:T(8,128)(2,1)S(1)}, u32[]{:S(2)}, u32[]{:S(2)}) collective-permute-start(bf16[8,2,128,256]{3,2,1,0:T(8,128)(2,1)} %all-to-all-done.1.mine_grad), channel_id=1, source_target_pairs={{0,16},{16,0},{32,48},{48,32},{64,80},{80,64},{96,112},{112,96},{1... | collective-permute-start | bytes 3145736 | tf_op jit(solution)/shard_map/ppermute | solution.py:296
  56.9 12.5 %all-to-all-start = ((s32[16,16,128]{2,1,0:T(8,128)}), s32[16,16,128]{2,1,0:T(8,128)S(1)}, u32[]{:S(2)}, u32[]{:S(2)}) async-start(s32[16,16,128]{2,1,0:T(8,128)} %bitcast.46), calls=%async_computation | async-start | bytes 262144 | tf_op jit(solution)/shard_map/all_to_all | solution.py:24
  60.4 5.0 %collective-permute-start.5 = (f32[16,1024]{1,0:T(8,128)S(1)}, f32[16,1024]{1,0:T(8,128)S(1)}, u32[]{:S(2)}, u32[]{:S(2)}) collective-permute-start(f32[16,1024]{1,0:T(8,128)S(1)} %get-tuple-element.29), channel_id=1, source_target_pairs={{0,4},{1,5},{2,6},{3,7},{4,8},{5,9},{6,10},{7,11},{8,12},{9,13},{1... | collective-permute-start | bytes 196616 | tf_op jit(solution)/shard_map/ppermute | solution.py:229
  61.8 3.7 %collective-permute-start.7 = (f32[16,1024]{1,0:T(8,128)S(1)}, f32[16,1024]{1,0:T(8,128)S(1)}, u32[]{:S(2)}, u32[]{:S(2)}) collective-permute-start(f32[16,1024]{1,0:T(8,128)S(1)} %get-tuple-element.30), channel_id=1, source_target_pairs={{0,12},{1,13},{2,14},{3,15},{4,0},{5,1},{6,2},{7,3},{8,4},{9,5},{1... | collective-permute-start | bytes 196616 | tf_op jit(solution)/shard_map/ppermute | solution.py:229
  63.3 4.9 %collective-permute-start.6 = (f32[16,1024]{1,0:T(8,128)S(1)}, f32[16,1024]{1,0:T(8,128)S(1)}, u32[]{:S(2)}, u32[]{:S(2)}) collective-permute-start(f32[16,1024]{1,0:T(8,128)S(1)} %get-tuple-element.31), channel_id=1, source_target_pairs={{0,8},{1,9},{2,10},{3,11},{4,12},{5,13},{6,14},{7,15},{8,0},{9,1},... | collective-permute-start | bytes 196616 | tf_op jit(solution)/shard_map/ppermute | solution.py:229
  69.4 0.7 copy-start.3
  70.1 1.0 copy-start.4
  83.0 142.9 %all-to-all-start.2 = ((bf16[16,272,1024]{2,1,0:T(8,128)(2,1)}), bf16[16,272,1024]{2,1,0:T(8,128)(2,1)}, u32[]{:S(2)}, u32[]{:S(2)}) async-start(bf16[16,272,1024]{2,1,0:T(8,128)(2,1)} %gather.1), calls=%async_computation.2 | async-start | bytes 17825792 | tf_op jit(solution)/shard_map/all_to_all | solution.py:24
  225.9 21.4 %all-to-all-start.3 = ((f32[8,16,1024]{2,1,0:T(8,128)}), f32[8,16,1024]{2,1,0:T(8,128)S(1)}, u32[]{:S(2)}, u32[]{:S(2)}) async-start(f32[8,16,1024]{2,1,0:T(8,128)} %broadcast_in_dim.7), calls=%async_computation.3 | async-start | bytes 1048576 | tf_op jit(solution)/shard_map/all_to_all | solution.py:303
  247.3 12.5 %collective-permute-start.8 = (f32[16,1024]{1,0:T(8,128)S(1)}, f32[16,1024]{1,0:T(8,128)S(1)}, u32[]{:S(2)}, u32[]{:S(2)}) collective-permute-start(f32[16,1024]{1,0:T(8,128)S(1)} %reduce_sum.19), channel_id=1, source_target_pairs={{0,16},{16,0},{32,48},{48,32},{64,80},{80,64},{96,112},{112,96},{1... | collective-permute-start | bytes 196616 | tf_op jit(solution)/shard_map/ppermute | solution.py:307
